TPU v7x, 256 devices: a whole 4x4x8 slice. The times are simulated.
256 devices in a mesh: dp: 64 (over x, z, y_hi), mp: 4 (over y_lo, core).
Axes of the slice: x: 4, y: 4 (y_hi: 2, y_lo: 2; y = y_hi * 2 + y_lo), z: 8, core: 2. Of those that a mesh axis runs over, the one named last changes fastest.
Arguments:
- media: bfloat16 [128, 8, 256, 1024], P('dp'), may hold values from -6 to 6
- latents: bfloat16 [64, 1024], replicated, may hold values from -6 to 6
- time_embed: bfloat16 [8, 1024], replicated, may hold values from -5 to 5
- media_gain: float32 [2, 1024], replicated, may hold values from 0.25 to 1.75
- latent_gain: float32 [2, 1024], replicated, may hold values from 0.25 to 1.75
- ffn_gain: float32 [2, 1024], replicated, may hold values from 0.25 to 1.75
- out_gain: float32 [1024], replicated, may hold values from 0.25 to 1.75
- w_query: bfloat16 [2, 1024, 512], P(None, 'dp', 'mp'), may hold values from -0.1875 to 0.1875
- w_key: bfloat16 [2, 1024, 512], P(None, 'dp', 'mp'), may hold values from -0.1875 to 0.1875
- w_value: bfloat16 [2, 1024, 512], P(None, 'dp', 'mp'), may hold values from -0.1875 to 0.1875
- w_out: bfloat16 [2, 512, 1024], P(None, 'mp', 'dp'), may hold values from -0.25 to 0.25
- w_up: bfloat16 [2, 1024, 4096], P(None, 'dp', 'mp'), may hold values from -0.1875 to 0.1875
- w_down: bfloat16 [2, 4096, 1024], P(None, 'mp', 'dp'), may hold values from -0.09375 to 0.09375
Outputs:
- resampled: bfloat16 [128, 64, 1024], P('dp')
All inputs are finite; a program needn't handle non-finite values.
Results may differ from a plain program's by a relative error of at most 0.013.
Values may be sent and summed in bfloat16 or wider, within the bound.
No kernel may reach another device: no remote copies, remote signals or barrier semaphores. Data moves between devices by JAX's collectives and lax.ppermute only.
A program may use at most 128 MiB of HBM per device.

v0:
```python
import functools

import jax
import jax.numpy as jnp
from jax import lax
from jax.experimental import pallas as pl
from jax.experimental.pallas import tpu as pltpu
from jax.sharding import Mesh, PartitionSpec as P

HEAD = 64
LAYERS = 2
CHUNK = 512
F32, BF16 = jnp.float32, jnp.bfloat16
DP = ("x", "z", "yh")
MP = ("yl", "c")


def params(mib=58):
    return pltpu.CompilerParams(vmem_limit_bytes=mib * 1024 * 1024)


def norm(v, g):
    center = v - jnp.mean(v, axis=-1, keepdims=True)
    spread = jnp.mean(center * center, axis=-1, keepdims=True)
    return center * lax.rsqrt(spread + 1e-05) * g


def dot(a, b, dims=((1,), (0,))):
    return lax.dot_general(a, b, (dims, ((), ())), preferred_element_type=F32)


def ring_pairs(n, step):
    return [(i, (i + step) % n) for i in range(n)]


def pack_kernel(q_ref, k_ref, v_ref, o_ref, u_ref, d_ref, first_ref, second_ref, down_ref, first, second, down, in_sems, out_sems):
    def tiles(ref, n):
        return [ref.at[n, :, pl.ds(k, 128)] for k in range(0, ref.shape[2], 128)]

    parts = [ref.at[n] for n in range(LAYERS) for ref in (q_ref, k_ref, v_ref, o_ref)]
    loads = [(block, first.at[k]) for k, block in enumerate(parts + tiles(u_ref, 0))]
    loads += [(block, second.at[k]) for k, block in enumerate(tiles(u_ref, 1) + tiles(d_ref, 1))]
    loads += [(d_ref.at[0], down)]
    loads = [pltpu.make_async_copy(src, dst, in_sems.at[k]) for k, (src, dst) in enumerate(loads)]
    for copy in loads:
        copy.start()
    for copy in loads:
        copy.wait()
    stores = [(src, dst.at[k]) for src, dst in ((first, first_ref), (second, second_ref)) for k in range(16)]
    stores += [(down, down_ref)]
    stores = [pltpu.make_async_copy(src, dst, out_sems.at[k]) for k, (src, dst) in enumerate(stores)]
    for copy in stores:
        copy.start()
    for copy in stores:
        copy.wait()


def pack(wq, wk, wv, out_t, up, down_t):
    anywhere = pl.BlockSpec(memory_space=pl.ANY)
    copies = jax.ShapeDtypeStruct((16, 16, 16, 128), BF16)
    return pl.pallas_call(
        pack_kernel,
        in_specs=[anywhere] * 6,
        out_specs=[anywhere] * 3,
        out_shape=[copies, copies, jax.ShapeDtypeStruct(down_t.shape[1:], BF16)],
        scratch_shapes=[
            pltpu.VMEM((16, 16, 128), BF16),
            pltpu.VMEM((16, 16, 128), BF16),
            pltpu.VMEM(down_t.shape[1:], BF16),
            pltpu.SemaphoreType.DMA((33,)),
            pltpu.SemaphoreType.DMA((33,)),
        ],
        compiler_params=params(),
        name="pack",
    )(wq, wk, wv, out_t, up, down_t)


def x_order(x, pieces):
    out = []
    for k, ref in enumerate(pieces):
        far = lax.rem(x + (0, 3, 1, 2, 2)[k], 4) * 16
        out.append((pl.ds(far + 8 if k == 4 else far, ref.shape[0]), ref))
    return out


def media_kernel(m_ref, t_ref, o_ref, buf, embed, in_sems, out_sems):
    samples, frames, patches, d = buf.shape
    tiles = [slice(k, k + 128) for k in range(0, d, 128)]
    ones = jnp.ones((d, 128), BF16)
    rows = 128
    places = [(i, f) for i in range(samples) for f in range(frames)]
    for k, p in enumerate(places):
        pltpu.make_async_copy(m_ref.at[p], buf.at[p], in_sems.at[k]).start()

    embed[...] = t_ref[...].astype(F32)

    def load(k):
        i, f = k // frames, lax.rem(k, frames)
        return pltpu.make_async_copy(m_ref.at[i, f], buf.at[i, f], in_sems.at[k])

    def store(k):
        i, f = k // frames, lax.rem(k, frames)
        return pltpu.make_async_copy(buf.at[i, f], o_ref.at[i, f], out_sems.at[k])

    def frame_of(k, _):
        i, f = k // frames, lax.rem(k, frames)
        load(k).wait()
        frame = embed[pl.ds(f, 1), :]
        shift = jnp.sum(frame, axis=-1, keepdims=True)
        for lo in range(0, patches, rows):
            at = slice(lo, lo + rows)
            mean = (dot(buf[i, f, at, :], ones) + shift) * (1.0 / d)
            spread = None
            for t in tiles:
                c = buf[i, f, at, t].astype(F32) + frame[:, t] - mean
                spread = c * c if spread is None else spread + c * c
            scale = lax.rsqrt(jnp.sum(spread, axis=-1, keepdims=True) * (1.0 / d) + 1e-05)
            for t in tiles:
                unit = (buf[i, f, at, t].astype(F32) + frame[:, t] - mean) * scale
                buf[i, f, at, t] = unit.astype(BF16)
        store(k).start()
        return 0

    lax.fori_loop(0, len(places), frame_of, 0)

    def stored(k, _):
        store(k).wait()
        return 0

    lax.fori_loop(0, len(places), stored, 0)


def norm_media(media, time_embed):
    s, f, p, d = media.shape
    anywhere = pl.BlockSpec(memory_space=pl.ANY)
    return pl.pallas_call(
        media_kernel,
        in_specs=[anywhere, pl.BlockSpec(memory_space=pltpu.VMEM)],
        out_specs=anywhere,
        out_shape=jax.ShapeDtypeStruct(media.shape, BF16),
        scratch_shapes=[
            pltpu.VMEM(media.shape, BF16),
            pltpu.VMEM(time_embed.shape, F32),
            pltpu.SemaphoreType.DMA((s * f,)),
            pltpu.SemaphoreType.DMA((s * f,)),
        ],
        compiler_params=params(),
        cost_estimate=pl.CostEstimate(flops=3 * 10**9, bytes_accessed=16 * 2**20, transcendentals=0),
        name="norm_media",
    )(media, time_embed).reshape(s, f * p, d)


def attention_kernel(layer, at_ref, m_ref, s_ref, g_ref, mg_ref, *refs):
    pieces, refs = refs[:4], refs[4:]
    updated = layer > 0
    if updated:
        mine_ref, theirs_ref, *refs = refs
    keep_ref, give_ref, new_ref, wide, kv_w, score, vals = refs
    samples, tokens, d = m_ref.shape
    lat = new_ref.shape[1]
    for rows, ref in x_order(at_ref[0], pieces):
        for k in range(4):
            wide[k, rows] = ref[:, k]
    gain = jnp.broadcast_to(mg_ref[layer : layer + 1, :], (128, d)).T

    def w(k):
        return wide[k].reshape(d, 128)

    for k in range(2):
        kv_w[:, k * 128 : (k + 1) * 128] = (w(1 + k).astype(F32) * gain).astype(BF16)
    core = at_ref[3]
    row = lax.broadcasted_iota(jnp.int32, (128, 2 * lat), 0) < HEAD
    col = lax.broadcasted_iota(jnp.int32, (128, 2 * lat), 1) < lat

    def fill(i, _):
        if updated:
            state = s_ref[i] + jnp.where(core == i, mine_ref[...].astype(F32), theirs_ref[...].astype(F32))
        else:
            state = s_ref[...].astype(F32)
        new_ref[i] = state
        ln = norm(state, g_ref[layer : layer + 1, :]).astype(BF16)
        q = (dot(ln, w(0)) * (HEAD**-0.5)).astype(BF16).astype(F32)
        qt = q.T
        q_bd = jnp.where(row == col, jnp.concatenate([qt, qt], axis=1), 0.0).astype(BF16)
        score[i, tokens:, :] = dot(dot(ln, w(1)).astype(BF16), q_bd)
        vals[i, tokens:, :] = dot(ln, w(2)).astype(BF16)
        for lo in range(0, tokens, CHUNK):
            at = slice(lo, lo + CHUNK)
            kv = dot(m_ref[i, at, :], kv_w[...]).astype(BF16)
            score[i, at, :] = dot(kv[:, :128], q_bd)
            vals[i, at, :] = kv[:, 128:]
        return 0

    lax.fori_loop(0, samples, fill, 0)

    def attend(i, _):
        sc = score[i]
        e = jnp.exp(sc - jnp.max(sc, axis=0, keepdims=True))
        probs = (e * (1.0 / jnp.sum(e, axis=0, keepdims=True))).astype(BF16)
        att = dot(probs, vals[i], ((0,), (0,)))
        mine = jnp.concatenate([att[:lat, :HEAD], att[lat:, HEAD:]], axis=1).astype(BF16)
        out = dot(mine, w(3), ((1,), (1,))).astype(BF16)

        @pl.when(core == i)
        def _():
            keep_ref[...] = out

        @pl.when(core != i)
        def _():
            give_ref[...] = out

        return 0

    lax.fori_loop(0, samples, attend, 0)


def attention(layer, places, media_normed, state, update, gain, media_gain, pieces):
    s, t, d = media_normed.shape
    lat = state.shape[-2]
    half = jax.ShapeDtypeStruct((lat, d), BF16)
    vmem = pl.BlockSpec(memory_space=pltpu.VMEM)
    return pl.pallas_call(
        functools.partial(attention_kernel, layer),
        in_specs=[pl.BlockSpec(memory_space=pltpu.SMEM)] + [vmem] * (8 + len(update)),
        out_specs=[vmem] * 3,
        out_shape=[half, half, jax.ShapeDtypeStruct((s, lat, d), F32)],
        scratch_shapes=[
            pltpu.VMEM((4, d // 16, 16, 128), BF16),
            pltpu.VMEM((d, 256), BF16),
            pltpu.VMEM((s, t + lat, 2 * lat), F32),
            pltpu.VMEM((s, t + lat, 128), BF16),
        ],
        compiler_params=params(24),
        cost_estimate=pl.CostEstimate(flops=6 * 10**9, bytes_accessed=10 * 2**20, transcendentals=10**6),
        name="attention",
    )(places, media_normed, state, gain, media_gain, *pieces, *update)


def ffn_kernel(layer, n_x, at_ref, s_ref, mine_ref, theirs_ref, g_ref, *refs):
    n_up = 5 if n_x == 16 else 4
    ups, downs, refs = refs[:n_up], refs[n_up:-6], refs[-6:]
    (keep_ref, give_ref, new_ref, u_ref, d_ref, o_ref) = refs
    rows, d = s_ref.shape
    hid = u_ref.shape[2]
    lat = rows // 2
    x, z, y, core = (at_ref[k] for k in range(4))
    tiles = [pl.ds(k, 128) for k in range(0, hid, 128)]
    order = x_order(x, ups)
    for at, ref in order:
        for k, tile in enumerate(tiles):
            u_ref[at, :, tile] = ref[:, k]
            if n_x == 16:
                d_ref[at, :, tile] = ref[:, 8 + k]
    for step, ref in zip((0, 7, 1, 6, 2, 5, 3, 4), downs):
        for i in range(4):
            far = lax.rem(x + (0, 3, 1, 2)[i], 4) * 8 + lax.rem(z + step, 8)
            for k in range(2):
                d_ref[far * 2 + (y if k == 0 else 1 - y)] = ref[i, k]
    here = pl.ds(pl.multiple_of(core * lat, lat), lat)
    there = pl.ds(pl.multiple_of((1 - core) * lat, lat), lat)
    new_ref[here, :] = s_ref[here, :] + mine_ref[...].astype(F32)
    new_ref[there, :] = s_ref[there, :] + theirs_ref[...].astype(F32)
    normed = norm(new_ref[...], g_ref[layer : layer + 1, :]).astype(BF16)
    up = dot(normed, u_ref[...].reshape(d, hid))
    hidden = (0.5 * up * (1.0 + lax.erf(up * (0.5**0.5)))).astype(BF16)
    o_ref[...] = dot(hidden, d_ref[...].reshape(d, hid), ((1,), (1,))).astype(BF16)
    keep_ref[...] = o_ref[here, :]
    give_ref[...] = o_ref[there, :]


def ffn(layer, places, state, update, gain, pieces):
    rows, d = state.shape
    vmem = pl.BlockSpec(memory_space=pltpu.VMEM)
    half = jax.ShapeDtypeStruct((rows // 2, d), BF16)
    return pl.pallas_call(
        functools.partial(ffn_kernel, layer, pieces[0].shape[1]),
        in_specs=[pl.BlockSpec(memory_space=pltpu.SMEM)] + [vmem] * (4 + len(pieces)),
        out_specs=[vmem] * 3,
        out_shape=[half, half, jax.ShapeDtypeStruct((rows, d), F32)],
        scratch_shapes=[
            pltpu.VMEM((d // 16, 16, 1024), BF16),
            pltpu.VMEM((d // 16, 16, 1024), BF16),
            pltpu.VMEM((rows, d), BF16),
        ],
        compiler_params=params(24),
        cost_estimate=pl.CostEstimate(flops=2 * 10**9, bytes_accessed=5 * 2**20, transcendentals=10**5),
        name="ffn",
    )(places, state, *update, gain, *pieces)


def x_ring(own):
    right, left = ring_pairs(4, 1), ring_pairs(4, -1)
    half = own.shape[0] // 2
    a, b = lax.ppermute(own, "x", right), lax.ppermute(own, "x", left)
    c, e = lax.ppermute(a[:half], "x", right), lax.ppermute(b[half:], "x", left)
    return own, a, b, c, e


def x_direct(own):
    return [own] + [lax.ppermute(own, "x", ring_pairs(4, step)) for step in (1, -1, 2)]


def z_ring(own):
    right, left = ring_pairs(8, 1), ring_pairs(8, -1)
    pieces, r, l = [own], own, own
    for k in range(4):
        r = lax.ppermute(r, "z", right)
        pieces.append(r)
        if k < 3:
            l = lax.ppermute(l, "z", left)
            pieces.append(l)
    return pieces


def down_pieces(own):
    other = lax.ppermute(own, "yh", [(0, 1), (1, 0)])
    line = x_direct(jnp.stack([own, other]))
    return z_ring(jnp.stack(line))


def total(keep, give):
    swap = [(0, 1), (1, 0)]
    got = lax.ppermute(give, "c", swap)
    half = (keep.astype(F32) + got.astype(F32)).astype(BF16)
    other = lax.ppermute(half, "yl", swap)
    full = (half.astype(F32) + other.astype(F32)).astype(BF16)
    return full, lax.ppermute(full, "c", swap)


def on_device(
    media, latents, time_embed, media_gain, latent_gain, ffn_gain, out_gain,
    w_query, w_key, w_value, w_out, w_up, w_down,
):
    samples, _, _, width = media.shape
    count = latents.shape[0]
    out_t = w_out.transpose(0, 2, 1)
    down_t = w_down.transpose(0, 2, 1)
    places = jnp.stack([lax.axis_index(k) for k in ("x", "z", "yh", "c")]).astype(jnp.int32)
    first, second, down = pack(w_query, w_key, w_value, out_t, w_up, down_t)
    first = lax.all_to_all(first, ("z", "yh"), 0, 0, tiled=True)
    down = down_pieces(down)
    heads = [x_direct(first[:, 4 * n : 4 * n + 4]) for n in range(LAYERS)]
    second = lax.all_to_all(second, ("z", "yh"), 0, 0, tiled=True)
    pieces = [(*x_direct(first[:, 8:]), *down), x_ring(second)]
    normed = norm_media(media, time_embed)
    state, update = latents, ()
    for n in range(LAYERS):
        keep, give, state = attention(n, places, normed, state, update, latent_gain, media_gain, heads[n])
        update = total(keep, give)
        rows = state.reshape(samples * count, width)
        keep, give, rows = ffn(n, places, rows, update, ffn_gain, pieces[n])
        state = rows.reshape(state.shape)
        update = total(keep, give)
    own = places[3] == 0
    added = jnp.stack([jnp.where(own, *update), jnp.where(own, *update[::-1])])
    return norm(state + added.astype(F32), out_gain).astype(BF16)


def solution(mesh):
    fine = Mesh(mesh.devices.reshape(4, 8, 2, 2, 2), ("x", "z", "yh", "yl", "c"))
    rows, cols = P(None, DP, MP), P(None, MP, DP)
    return jax.shard_map(
        on_device,
        mesh=fine,
        in_specs=(P(DP), P(), P(), P(), P(), P(), P(), rows, rows, rows, cols, rows, cols),
        out_specs=P(DP),
        check_vma=False,
    )
```

profile of v0, /device:TPU:1, one launch (start us, length us, event | category | flops | bytes accessed | tf_op | source)
XLA Modules:
  0.0 180.9 jit_solution(17246630849414543974)
XLA Ops:
  0.0 2.9 %pack.1 = (bf16[16,16,16,128]{3,2,1,0:T(8,128)(2,1)}, bf16[16,16,16,128]{3,2,1,0:T(8,128)(2,1)}, bf16[16,1024]{1,0:T(8,128)(2,1)}) custom-call(bf16[2,16,128]{2,1,0:T(8,128)(2,1)} %q_ref.1, bf16[2,16,128]{2,1,0:T(8,128)(2,1)} %k_ref.1, bf16[2,16,128]{2,1,0:T(8,128)(2,1)} %v_ref.1, bf16[2,16,128]{2,1,0:T(8,128)(2,1)} %bitcast.40, bf16[2,16,1024]{2,1,0:T(8,128)(2,1)} %u_ref.1, ...), custom_call_target="tpu_custom_call" | custom-call | tf_op jit(solution)/shard_map/pack/pallas_call | solution.py:61
  2.9 11.8 %all-to-all-start = ((bf16[16,16,16,128]{3,2,1,0:T(8,128)(2,1)}), bf16[16,16,16,128]{3,2,1,0:T(8,128)(2,1)S(1)}, u32[]{:S(2)}, u32[]{:S(2)}) async-start(bf16[16,16,16,128]{3,2,1,0:T(8,128)(2,1)} %get-tuple-element.20), calls=%async_computation | async-start | bytes 2097152 | tf_op jit(solution)/shard_map/all_to_all | solution.py:340
  14.7 2.9 %collective-permute-start.9 = (bf16[16,1024]{1,0:T(8,128)(2,1)}, bf16[16,1024]{1,0:T(8,128)(2,1)S(1)}, u32[]{:S(2)}, u32[]{:S(2)}) collective-permute-start(bf16[16,1024]{1,0:T(8,128)(2,1)} %get-tuple-element.24), channel_id=1, source_target_pairs={{0,4},{4,0},{1,5},{5,1},{2,6},{6,2},{3,7},{7,3},{8,12},{12,8},{9,1... | collective-permute-start | bytes 98312 | tf_op jit(solution)/shard_map/ppermute | solution.py:316
  17.5 2.2 %collective-permute-done.9 = bf16[16,1024]{1,0:T(8,128)(2,1)S(1)} collective-permute-done((bf16[16,1024]{1,0:T(8,128)(2,1)}, bf16[16,1024]{1,0:T(8,128)(2,1)S(1)}, u32[]{:S(2)}, u32[]{:S(2)}) %collective-permute-start.9) | collective-permute-done | bytes 32800 | tf_op jit(solution)/shard_map/ppermute | solution.py:316
  19.7 0.8 fusion.1
  20.5 1.3 collective-permute-start.10
  21.8 1.5 collective-permute-start.11
  23.3 1.5 collective-permute-start.12
  24.9 0.3 collective-permute-done.10
  25.2 3.1 %collective-permute-done.12 = bf16[2,16,1024]{2,1,0:T(8,128)(2,1)S(1)} collective-permute-done((bf16[2,16,1024]{2,1,0:T(8,128)(2,1)S(1)}, bf16[2,16,1024]{2,1,0:T(8,128)(2,1)S(1)}, u32[]{:S(2)}, u32[]{:S(2)}) %collective-permute-start.12) | collective-permute-done | bytes 65568 | tf_op jit(solution)/shard_map/ppermute | solution.py:300
  28.3 1.0 collective-permute-start.13
  29.3 12.3 %all-to-all-done = bf16[16,16,16,128]{3,2,1,0:T(8,128)(2,1)S(1)} async-done(((bf16[16,16,16,128]{3,2,1,0:T(8,128)(2,1)}), bf16[16,16,16,128]{3,2,1,0:T(8,128)(2,1)S(1)}, u32[]{:S(2)}, u32[]{:S(2)}) %all-to-all-start) | async-done | bytes 1048608 | tf_op jit(solution)/shard_map/all_to_all | solution.py:340
  41.6 6.2 %all-to-all-start.1 = ((bf16[16,16,16,128]{3,2,1,0:T(8,128)(2,1)}), bf16[16,16,16,128]{3,2,1,0:T(8,128)(2,1)S(1)}, u32[]{:S(2)}, u32[]{:S(2)}) async-start(bf16[16,16,16,128]{3,2,1,0:T(8,128)(2,1)} %get-tuple-element.31), calls=%async_computation.1 | async-start | bytes 2097152 | tf_op jit(solution)/shard_map/all_to_all | solution.py:343
  47.9 1.3 collective-permute-start
  49.2 1.5 collective-permute-start.1
  50.7 1.5 collective-permute-start.2
  52.2 11.8 %norm_media.1 = bf16[2,8,256,1024]{3,2,1,0:T(8,128)(2,1)} custom-call(bf16[2,8,256,1024]{3,2,1,0:T(8,128)(2,1)} %m_ref.1, bf16[8,1024]{1,0:T(8,128)(2,1)} %t_ref.1), custom_call_target="tpu_custom_call" | custom-call | flops 3000000000 | bytes 16777216 | tf_op jit(solution)/shard_map/norm_media/pallas_call | solution.py:136
  64.0 2.7 %collective-permute-start.14 = (bf16[4,2,16,1024]{3,2,1,0:T(8,128)(2,1)S(1)}, bf16[4,2,16,1024]{3,2,1,0:T(8,128)(2,1)S(1)}, u32[]{:S(2)}, u32[]{:S(2)}) collective-permute-start(bf16[4,2,16,1024]{3,2,1,0:T(8,128)(2,1)S(1)} %pad_maximum_fusion.refs_4_), channel_id=1, source_target_pairs={{0,56},{8,0},{16,8},{24,16},{32,24},{40,32},{48,40},{56,48},{1,57}... | collective-permute-start | bytes 786440 | tf_op jit(solution)/shard_map/ppermute | solution.py:310
  66.7 3.4 %copy-done = bf16[2,8,256,1024]{3,2,1,0:T(8,128)(2,1)S(1)} copy-done((bf16[2,8,256,1024]{3,2,1,0:T(8,128)(2,1)S(1)}, bf16[2,8,256,1024]{3,2,1,0:T(8,128)(2,1)}, u32[]{:S(2)}) %copy-start) | copy-done | bytes 8388632
  70.1 9.0 %attention.2 = (bf16[64,1024]{1,0:T(8,128)(2,1)S(1)}, bf16[64,1024]{1,0:T(8,128)(2,1)S(1)}, f32[2,64,1024]{2,1,0:T(8,128)S(1)}) custom-call(s32[4]{0:T(128)S(1)} %pad_add_fusion.at_ref, bf16[2,2048,1024]{2,1,0:T(8,128)(2,1)S(1)} %bitcast.28, bf16[64,1024]{1,0:T(8,128)(2,1)S(1)} %copy-done.2, f32[2,1024]{1,0:T(2,128)S(1)} %copy-done.3, ...), custom_call_target="tpu_custom_call" | custom-call | flops 6000000000 | bytes 10485760 | tf_op jit(solution)/shard_map/attention/pallas_call | solution.py:222
  79.1 3.3 %collective-permute-start.3 = (bf16[64,1024]{1,0:T(8,128)(2,1)S(1)}, bf16[64,1024]{1,0:T(8,128)(2,1)S(1)}, u32[]{:S(2)}, u32[]{:S(2)}) collective-permute-start(bf16[64,1024]{1,0:T(8,128)(2,1)S(1)} %get-tuple-element.23), channel_id=1, source_target_pairs={{0,1},{1,0},{2,3},{3,2},{4,5},{5,4},{6,7},{7,6},{8,9},{9,8},{10,11... | collective-permute-start | bytes 393224 | tf_op jit(solution)/shard_map/ppermute | solution.py:323
  82.3 2.9 %collective-permute-start.16 = (bf16[4,2,16,1024]{3,2,1,0:T(8,128)(2,1)S(1)}, bf16[4,2,16,1024]{3,2,1,0:T(8,128)(2,1)S(1)}, u32[]{:S(2)}, u32[]{:S(2)}) collective-permute-start(bf16[4,2,16,1024]{3,2,1,0:T(8,128)(2,1)S(1)} %collective-permute-done.14.refs_6_), channel_id=1, source_target_pairs={{0,56},{8,0},{16,8},{24,16},{32,24},{40,32},{48,40},{56,48},{1,57}... | collective-permute-start | bytes 786440 | tf_op jit(solution)/shard_map/ppermute | solution.py:310
  85.3 0.4 collective-permute-start.6
  85.8 2.3 %collective-permute-start.7 = (bf16[16,8,16,128]{3,2,1,0:T(8,128)(2,1)S(1)}, bf16[16,8,16,128]{3,2,1,0:T(8,128)(2,1)S(1)}, u32[]{:S(2)}, u32[]{:S(2)}) collective-permute-start(bf16[16,8,16,128]{3,2,1,0:T(8,128)(2,1)S(1)} %slice.21.refs_0_), channel_id=1, source_target_pairs={{0,192},{64,0},{128,64},{192,128},{1,193},{65,1},{129,65},{193,129... | collective-permute-start | bytes 1572872 | tf_op jit(solution)/shard_map/ppermute | solution.py:300
  88.1 0.3 collective-permute-start.8
  88.4 2.2 %collective-permute-done.16.refs_8_ = bf16[4,2,16,1024]{3,2,1,0:T(8,128)(2,1)S(1)} collective-permute-done((bf16[4,2,16,1024]{3,2,1,0:T(8,128)(2,1)S(1)}, bf16[4,2,16,1024]{3,2,1,0:T(8,128)(2,1)S(1)}, u32[]{:S(2)}, u32[]{:S(2)}) %collective-permute-start.16) | collective-permute-done | bytes 262176 | tf_op jit(solution)/shard_map/ppermute | solution.py:310
  90.7 0.5 collective-permute-start.4
  91.1 2.7 %collective-permute-done.17.refs_9_ = bf16[4,2,16,1024]{3,2,1,0:T(8,128)(2,1)S(1)} collective-permute-done((bf16[4,2,16,1024]{3,2,1,0:T(8,128)(2,1)S(1)}, bf16[4,2,16,1024]{3,2,1,0:T(8,128)(2,1)S(1)}, u32[]{:S(2)}, u32[]{:S(2)}) %collective-permute-start.17) | collective-permute-done | bytes 262176 | tf_op jit(solution)/shard_map/ppermute | solution.py:307
  93.8 0.7 collective-permute-start.18
  94.8 0.5 collective-permute-start.19
  95.3 4.9 %collective-permute-done.18.refs_10_ = bf16[4,2,16,1024]{3,2,1,0:T(8,128)(2,1)S(1)} collective-permute-done((bf16[4,2,16,1024]{3,2,1,0:T(8,128)(2,1)S(1)}, bf16[4,2,16,1024]{3,2,1,0:T(8,128)(2,1)S(1)}, u32[]{:S(2)}, u32[]{:S(2)}) %collective-permute-start.18) | collective-permute-done | bytes 262176 | tf_op jit(solution)/shard_map/ppermute | solution.py:310
  100.2 2.3 %collective-permute-start.5 = (bf16[64,1024]{1,0:T(8,128)(2,1)S(1)}, bf16[64,1024]{1,0:T(8,128)(2,1)S(1)}, u32[]{:S(2)}, u32[]{:S(2)}) collective-permute-start(bf16[64,1024]{1,0:T(8,128)(2,1)S(1)} %add_convert_fusion.6.mine_ref), channel_id=1, source_target_pairs={{0,1},{1,0},{2,3},{3,2},{4,5},{5,4},{6,7},{7,6},{8,9},{9,8},{10,11... | collective-permute-start | bytes 393224 | tf_op jit(solution)/shard_map/ppermute | solution.py:327
  102.5 0.4 collective-permute-done.19.refs_11_
  102.9 7.4 %collective-permute-done.8.refs_3_ = bf16[16,8,16,128]{3,2,1,0:T(8,128)(2,1)S(1)} collective-permute-done((bf16[16,8,16,128]{3,2,1,0:T(8,128)(2,1)S(1)}, bf16[16,8,16,128]{3,2,1,0:T(8,128)(2,1)S(1)}, u32[]{:S(2)}, u32[]{:S(2)}) %collective-permute-start.8) | collective-permute-done | bytes 524320 | tf_op jit(solution)/shard_map/ppermute | solution.py:300
  110.3 2.4 %ffn.2 = (bf16[64,1024]{1,0:T(8,128)(2,1)S(1)}, bf16[64,1024]{1,0:T(8,128)(2,1)S(1)}, f32[128,1024]{1,0:T(8,128)S(1)}) custom-call(s32[4]{0:T(128)S(1)} %pad_add_fusion.at_ref, f32[128,1024]{1,0:T(8,128)S(1)} %bitcast.31, bf16[64,1024]{1,0:T(8,128)(2,1)S(1)} %add_convert_fusion.6.mine_ref, bf16[64,1024]{1,0:T(8,128)(2,1)S(1)} %collective-permute-done.5.theirs_ref, ...), custom_call_target="tpu_custom_call" | custom-call | flops 2000000000 | bytes 5242880 | tf_op jit(solution)/shard_map/ffn/pallas_call | solution.py:275
  112.7 2.1 %collective-permute-start.23 = (bf16[64,1024]{1,0:T(8,128)(2,1)S(1)}, bf16[64,1024]{1,0:T(8,128)(2,1)S(1)}, u32[]{:S(2)}, u32[]{:S(2)}) collective-permute-start(bf16[64,1024]{1,0:T(8,128)(2,1)S(1)} %get-tuple-element.27), channel_id=1, source_target_pairs={{0,1},{1,0},{2,3},{3,2},{4,5},{5,4},{6,7},{7,6},{8,9},{9,8},{10,11... | collective-permute-start | bytes 393224 | tf_op jit(solution)/shard_map/ppermute | solution.py:323
  114.7 1.0 collective-permute-done.23
  115.8 0.5 collective-permute-start.24
  116.3 0.6 collective-permute-start.20
  116.9 2.1 %collective-permute-start.21 = (bf16[16,4,16,128]{3,2,1,0:T(8,128)(2,1)S(1)}, bf16[16,4,16,128]{3,2,1,0:T(8,128)(2,1)S(1)}, u32[]{:S(2)}, u32[]{:S(2)}) collective-permute-start(bf16[16,4,16,128]{3,2,1,0:T(8,128)(2,1)S(1)} %get-tuple-element.35.refs_0_), channel_id=1, source_target_pairs={{0,192},{64,0},{128,64},{192,128},{1,193},{65,1},{129,65},{193,129... | collective-permute-start | bytes 786440 | tf_op jit(solution)/shard_map/ppermute | solution.py:300
  119.0 1.2 collective-permute-start.22
  120.2 0.9 collective-permute-start.29
  121.0 2.2 %collective-permute-start.30 = (bf16[16,16,16,128]{3,2,1,0:T(8,128)(2,1)S(1)}, bf16[16,16,16,128]{3,2,1,0:T(8,128)(2,1)S(1)}, u32[]{:S(2)}, u32[]{:S(2)}) collective-permute-start(bf16[16,16,16,128]{3,2,1,0:T(8,128)(2,1)S(1)} %all-to-all-done.1.refs_0_), channel_id=1, source_target_pairs={{0,192},{64,0},{128,64},{192,128},{1,193},{65,1},{129,65},{193,129... | collective-permute-start | bytes 3145736 | tf_op jit(solution)/shard_map/ppermute | solution.py:294
  123.2 1.5 collective-permute-done.20.refs_1_
  124.7 3.6 %collective-permute-start.25 = (bf16[64,1024]{1,0:T(8,128)(2,1)S(1)}, bf16[64,1024]{1,0:T(8,128)(2,1)S(1)}, u32[]{:S(2)}, u32[]{:S(2)}) collective-permute-start(bf16[64,1024]{1,0:T(8,128)(2,1)S(1)} %add_convert_fusion.4.refs_4_), channel_id=1, source_target_pairs={{0,1},{1,0},{2,3},{3,2},{4,5},{5,4},{6,7},{7,6},{8,9},{9,8},{10,11... | collective-permute-start | bytes 393224 | tf_op jit(solution)/shard_map/ppermute | solution.py:327
  128.4 3.2 %collective-permute-done.22.refs_3_ = bf16[16,4,16,128]{3,2,1,0:T(8,128)(2,1)S(1)} collective-permute-done((bf16[16,4,16,128]{3,2,1,0:T(8,128)(2,1)S(1)}, bf16[16,4,16,128]{3,2,1,0:T(8,128)(2,1)S(1)}, u32[]{:S(2)}, u32[]{:S(2)}) %collective-permute-start.22) | collective-permute-done | bytes 262176 | tf_op jit(solution)/shard_map/ppermute | solution.py:300
  131.6 3.4 %copy-done.1 = bf16[2,8,256,1024]{3,2,1,0:T(8,128)(2,1)S(1)} copy-done((bf16[2,8,256,1024]{3,2,1,0:T(8,128)(2,1)S(1)}, bf16[2,8,256,1024]{3,2,1,0:T(8,128)(2,1)}, u32[]{:S(2)}) %copy-start.1) | copy-done | bytes 8388632
  135.0 9.0 %attention.3 = (bf16[64,1024]{1,0:T(8,128)(2,1)S(1)}, bf16[64,1024]{1,0:T(8,128)(2,1)S(1)}, f32[2,64,1024]{2,1,0:T(8,128)S(1)}) custom-call(s32[4]{0:T(128)S(1)} %pad_add_fusion.at_ref, bf16[2,2048,1024]{2,1,0:T(8,128)(2,1)S(1)} %bitcast.29, f32[2,64,1024]{2,1,0:T(8,128)S(1)} %bitcast.32, f32[2,1024]{1,0:T(2,128)S(1)} %copy-done.3, f32[2,1024]{1,0:T(2,128)S(1)} %copy-done.4, ...), custom_call_target="tpu_custom_call" | custom-call | flops 6000000000 | bytes 10485760 | tf_op jit(solution)/shard_map/attention/pallas_call | solution.py:222
  144.0 2.7 %collective-permute-start.26 = (bf16[64,1024]{1,0:T(8,128)(2,1)S(1)}, bf16[64,1024]{1,0:T(8,128)(2,1)S(1)}, u32[]{:S(2)}, u32[]{:S(2)}) collective-permute-start(bf16[64,1024]{1,0:T(8,128)(2,1)S(1)} %get-tuple-element.30), channel_id=1, source_target_pairs={{0,1},{1,0},{2,3},{3,2},{4,5},{5,4},{6,7},{7,6},{8,9},{9,8},{10,11... | collective-permute-start | bytes 393224 | tf_op jit(solution)/shard_map/ppermute | solution.py:323
  146.7 6.1 %collective-permute-done.29.refs_1_ = bf16[16,16,16,128]{3,2,1,0:T(8,128)(2,1)S(1)} collective-permute-done((bf16[16,16,16,128]{3,2,1,0:T(8,128)(2,1)S(1)}, bf16[16,16,16,128]{3,2,1,0:T(8,128)(2,1)S(1)}, u32[]{:S(2)}, u32[]{:S(2)}) %collective-permute-start.29) | collective-permute-done | bytes 1048608 | tf_op jit(solution)/shard_map/ppermute | solution.py:294
  153.0 2.7 %collective-permute-start.32 = (bf16[8,16,16,128]{3,2,1,0:T(8,128)(2,1)S(1)}, bf16[8,16,16,128]{3,2,1,0:T(8,128)(2,1)S(1)}, u32[]{:S(2)}, u32[]{:S(2)}) collective-permute-start(bf16[8,16,16,128]{3,2,1,0:T(8,128)(2,1)S(1)} %slice.24), channel_id=1, source_target_pairs={{0,192},{64,0},{128,64},{192,128},{1,193},{65,1},{129,65},{193,129... | collective-permute-start | bytes 1572872 | tf_op jit(solution)/shard_map/ppermute | solution.py:295
  155.8 1.1 collective-permute-start.27
  156.9 3.1 %collective-permute-done.27 = bf16[64,1024]{1,0:T(8,128)(2,1)S(1)} collective-permute-done((bf16[64,1024]{1,0:T(8,128)(2,1)S(1)}, bf16[64,1024]{1,0:T(8,128)(2,1)S(1)}, u32[]{:S(2)}, u32[]{:S(2)}) %collective-permute-start.27) | collective-permute-done | bytes 131104 | tf_op jit(solution)/shard_map/ppermute | solution.py:325
  160.0 3.0 %collective-permute-start.28 = (bf16[64,1024]{1,0:T(8,128)(2,1)S(1)}, bf16[64,1024]{1,0:T(8,128)(2,1)S(1)}, u32[]{:S(2)}, u32[]{:S(2)}) collective-permute-start(bf16[64,1024]{1,0:T(8,128)(2,1)S(1)} %add_convert_fusion.2.mine_ref), channel_id=1, source_target_pairs={{0,1},{1,0},{2,3},{3,2},{4,5},{5,4},{6,7},{7,6},{8,9},{9,8},{10,11... | collective-permute-start | bytes 393224 | tf_op jit(solution)/shard_map/ppermute | solution.py:327
  163.0 1.0 collective-permute-done.28.theirs_ref
  164.0 2.1 %collective-permute-done.31.refs_3_ = bf16[8,16,16,128]{3,2,1,0:T(8,128)(2,1)S(1)} collective-permute-done((bf16[8,16,16,128]{3,2,1,0:T(8,128)(2,1)S(1)}, bf16[8,16,16,128]{3,2,1,0:T(8,128)(2,1)S(1)}, u32[]{:S(2)}, u32[]{:S(2)}) %collective-permute-start.31) | collective-permute-done | bytes 524320 | tf_op jit(solution)/shard_map/ppermute | solution.py:295
  166.1 2.7 %ffn.3 = (bf16[64,1024]{1,0:T(8,128)(2,1)S(1)}, bf16[64,1024]{1,0:T(8,128)(2,1)S(1)}, f32[128,1024]{1,0:T(8,128)S(1)}) custom-call(s32[4]{0:T(128)S(1)} %pad_add_fusion.at_ref, f32[128,1024]{1,0:T(8,128)S(1)} %bitcast.33, bf16[64,1024]{1,0:T(8,128)(2,1)S(1)} %add_convert_fusion.2.mine_ref, bf16[64,1024]{1,0:T(8,128)(2,1)S(1)} %collective-permute-done.28.theirs_ref, ...), custom_call_target="tpu_custom_call" | custom-call | flops 2000000000 | bytes 5242880 | tf_op jit(solution)/shard_map/ffn/pallas_call | solution.py:275
  168.8 2.4 %collective-permute-start.33 = (bf16[64,1024]{1,0:T(8,128)(2,1)S(1)}, bf16[64,1024]{1,0:T(8,128)(2,1)S(1)}, u32[]{:S(2)}, u32[]{:S(2)}) collective-permute-start(bf16[64,1024]{1,0:T(8,128)(2,1)S(1)} %get-tuple-element.34), channel_id=1, source_target_pairs={{0,1},{1,0},{2,3},{3,2},{4,5},{5,4},{6,7},{7,6},{8,9},{9,8},{10,11... | collective-permute-start | bytes 393224 | tf_op jit(solution)/shard_map/ppermute | solution.py:323
  171.3 1.0 collective-permute-done.33
  172.3 1.1 collective-permute-start.34
  173.4 3.7 %collective-permute-done.34 = bf16[64,1024]{1,0:T(8,128)(2,1)S(1)} collective-permute-done((bf16[64,1024]{1,0:T(8,128)(2,1)S(1)}, bf16[64,1024]{1,0:T(8,128)(2,1)S(1)}, u32[]{:S(2)}, u32[]{:S(2)}) %collective-permute-start.34) | collective-permute-done | bytes 131104 | tf_op jit(solution)/shard_map/ppermute | solution.py:325
  177.1 1.3 collective-permute-start.35
  178.4 1.0 collective-permute-done.35
  180.0 0.9 multiply_convert_fusion
  (56 shorter events, 1.5 us)
Async XLA Ops:
  2.9 38.7 %all-to-all-start = ((bf16[16,16,16,128]{3,2,1,0:T(8,128)(2,1)}), bf16[16,16,16,128]{3,2,1,0:T(8,128)(2,1)S(1)}, u32[]{:S(2)}, u32[]{:S(2)}) async-start(bf16[16,16,16,128]{3,2,1,0:T(8,128)(2,1)} %get-tuple-element.20), calls=%async_computation | async-start | bytes 2097152 | tf_op jit(solution)/shard_map/all_to_all | solution.py:340
  14.7 5.1 %collective-permute-start.9 = (bf16[16,1024]{1,0:T(8,128)(2,1)}, bf16[16,1024]{1,0:T(8,128)(2,1)S(1)}, u32[]{:S(2)}, u32[]{:S(2)}) collective-permute-start(bf16[16,1024]{1,0:T(8,128)(2,1)} %get-tuple-element.24), channel_id=1, source_target_pairs={{0,4},{4,0},{1,5},{5,1},{2,6},{6,2},{3,7},{7,3},{8,12},{12,8},{9,1... | collective-permute-start | bytes 98312 | tf_op jit(solution)/shard_map/ppermute | solution.py:316
  20.5 4.7 %collective-permute-start.10 = (bf16[2,16,1024]{2,1,0:T(8,128)(2,1)S(1)}, bf16[2,16,1024]{2,1,0:T(8,128)(2,1)S(1)}, u32[]{:S(2)}, u32[]{:S(2)}) collective-permute-start(bf16[2,16,1024]{2,1,0:T(8,128)(2,1)S(1)} %get-tuple-element.40), channel_id=1, source_target_pairs={{0,64},{64,128},{128,192},{192,0},{1,65},{65,129},{129,193},{193,1... | collective-permute-start | bytes 196616 | tf_op jit(solution)/shard_map/ppermute | solution.py:300
  21.8 3.4 %collective-permute-start.11 = (bf16[2,16,1024]{2,1,0:T(8,128)(2,1)S(1)}, bf16[2,16,1024]{2,1,0:T(8,128)(2,1)S(1)}, u32[]{:S(2)}, u32[]{:S(2)}) collective-permute-start(bf16[2,16,1024]{2,1,0:T(8,128)(2,1)S(1)} %get-tuple-element.40), channel_id=1, source_target_pairs={{0,192},{64,0},{128,64},{192,128},{1,193},{65,1},{129,65},{193,129... | collective-permute-start | bytes 196616 | tf_op jit(solution)/shard_map/ppermute | solution.py:300
  23.3 5.0 %collective-permute-start.12 = (bf16[2,16,1024]{2,1,0:T(8,128)(2,1)S(1)}, bf16[2,16,1024]{2,1,0:T(8,128)(2,1)S(1)}, u32[]{:S(2)}, u32[]{:S(2)}) collective-permute-start(bf16[2,16,1024]{2,1,0:T(8,128)(2,1)S(1)} %get-tuple-element.40), channel_id=1, source_target_pairs={{0,128},{64,192},{128,0},{192,64},{1,129},{65,193},{129,1},{193,65... | collective-permute-start | bytes 196616 | tf_op jit(solution)/shard_map/ppermute | solution.py:300
  28.3 38.3 %collective-permute-start.13 = (bf16[4,2,16,1024]{3,2,1,0:T(8,128)(2,1)S(1)}, bf16[4,2,16,1024]{3,2,1,0:T(8,128)(2,1)S(1)}, u32[]{:S(2)}, u32[]{:S(2)}) collective-permute-start(bf16[4,2,16,1024]{3,2,1,0:T(8,128)(2,1)S(1)} %pad_maximum_fusion.refs_4_), channel_id=1, source_target_pairs={{0,8},{8,16},{16,24},{24,32},{32,40},{40,48},{48,56},{56,0},{1,9},... | collective-permute-start | bytes 786440 | tf_op jit(solution)/shard_map/ppermute | solution.py:307
  41.6 78.6 %all-to-all-start.1 = ((bf16[16,16,16,128]{3,2,1,0:T(8,128)(2,1)}), bf16[16,16,16,128]{3,2,1,0:T(8,128)(2,1)S(1)}, u32[]{:S(2)}, u32[]{:S(2)}) async-start(bf16[16,16,16,128]{3,2,1,0:T(8,128)(2,1)} %get-tuple-element.31), calls=%async_computation.1 | async-start | bytes 2097152 | tf_op jit(solution)/shard_map/all_to_all | solution.py:343
  47.9 18.8 %copy-start.2 = (bf16[64,1024]{1,0:T(8,128)(2,1)S(1)}, bf16[64,1024]{1,0:T(8,128)(2,1)}, u32[]{:S(2)}) copy-start(bf16[64,1024]{1,0:T(8,128)(2,1)} %s_ref.1) | copy-start | bytes 393220
  47.9 18.8 %copy-start.3 = (f32[2,1024]{1,0:T(2,128)S(1)}, f32[2,1024]{1,0:T(2,128)}, u32[]{:S(2)}) copy-start(f32[2,1024]{1,0:T(2,128)} %g_ref.6) | copy-start | bytes 24580
  47.9 18.8 %copy-start.4 = (f32[2,1024]{1,0:T(2,128)S(1)}, f32[2,1024]{1,0:T(2,128)}, u32[]{:S(2)}) copy-start(f32[2,1024]{1,0:T(2,128)} %mg_ref.3) | copy-start | bytes 24580
  47.9 18.7 %collective-permute-start = (bf16[16,4,16,128]{3,2,1,0:T(8,128)(2,1)S(1)}, bf16[16,4,16,128]{3,2,1,0:T(8,128)(2,1)S(1)}, u32[]{:S(2)}, u32[]{:S(2)}) collective-permute-start(bf16[16,4,16,128]{3,2,1,0:T(8,128)(2,1)S(1)} %get-tuple-element.36.refs_0_), channel_id=1, source_target_pairs={{0,64},{64,128},{128,192},{192,0},{1,65},{65,129},{129,193},{193,1... | collective-permute-start | bytes 786440 | tf_op jit(solution)/shard_map/ppermute | solution.py:300
  49.2 17.4 %collective-permute-start.1 = (bf16[16,4,16,128]{3,2,1,0:T(8,128)(2,1)S(1)}, bf16[16,4,16,128]{3,2,1,0:T(8,128)(2,1)S(1)}, u32[]{:S(2)}, u32[]{:S(2)}) collective-permute-start(bf16[16,4,16,128]{3,2,1,0:T(8,128)(2,1)S(1)} %get-tuple-element.36.refs_0_), channel_id=1, source_target_pairs={{0,192},{64,0},{128,64},{192,128},{1,193},{65,1},{129,65},{193,129... | collective-permute-start | bytes 786440 | tf_op jit(solution)/shard_map/ppermute | solution.py:300
  50.7 16.0 %collective-permute-start.2 = (bf16[16,4,16,128]{3,2,1,0:T(8,128)(2,1)S(1)}, bf16[16,4,16,128]{3,2,1,0:T(8,128)(2,1)S(1)}, u32[]{:S(2)}, u32[]{:S(2)}) collective-permute-start(bf16[16,4,16,128]{3,2,1,0:T(8,128)(2,1)S(1)} %get-tuple-element.36.refs_0_), channel_id=1, source_target_pairs={{0,128},{64,192},{128,0},{192,64},{1,129},{65,193},{129,1},{193,65... | collective-permute-start | bytes 786440 | tf_op jit(solution)/shard_map/ppermute | solution.py:300
  64.0 18.4 %collective-permute-start.14 = (bf16[4,2,16,1024]{3,2,1,0:T(8,128)(2,1)S(1)}, bf16[4,2,16,1024]{3,2,1,0:T(8,128)(2,1)S(1)}, u32[]{:S(2)}, u32[]{:S(2)}) collective-permute-start(bf16[4,2,16,1024]{3,2,1,0:T(8,128)(2,1)S(1)} %pad_maximum_fusion.refs_4_), channel_id=1, source_target_pairs={{0,56},{8,0},{16,8},{24,16},{32,24},{40,32},{48,40},{56,48},{1,57}... | collective-permute-start | bytes 786440 | tf_op jit(solution)/shard_map/ppermute | solution.py:310
  66.6 18.7 %collective-permute-start.15 = (bf16[4,2,16,1024]{3,2,1,0:T(8,128)(2,1)S(1)}, bf16[4,2,16,1024]{3,2,1,0:T(8,128)(2,1)S(1)}, u32[]{:S(2)}, u32[]{:S(2)}) collective-permute-start(bf16[4,2,16,1024]{3,2,1,0:T(8,128)(2,1)S(1)} %collective-permute-done.13.refs_5_), channel_id=1, source_target_pairs={{0,8},{8,16},{16,24},{24,32},{32,40},{40,48},{48,56},{56,0},{1,9},... | collective-permute-start | bytes 786440 | tf_op jit(solution)/shard_map/ppermute | solution.py:307
  66.7 3.4 %copy-start = (bf16[2,8,256,1024]{3,2,1,0:T(8,128)(2,1)S(1)}, bf16[2,8,256,1024]{3,2,1,0:T(8,128)(2,1)}, u32[]{:S(2)}) copy-start(bf16[2,8,256,1024]{3,2,1,0:T(8,128)(2,1)} %norm_media.1) | copy-start | bytes 25165828
  70.1 40.2 %copy-start.5 = (f32[2,1024]{1,0:T(2,128)S(1)}, f32[2,1024]{1,0:T(2,128)}, u32[]{:S(2)}) copy-start(f32[2,1024]{1,0:T(2,128)} %g_ref.7) | copy-start | bytes 24580
  79.1 9.0 %collective-permute-start.3 = (bf16[64,1024]{1,0:T(8,128)(2,1)S(1)}, bf16[64,1024]{1,0:T(8,128)(2,1)S(1)}, u32[]{:S(2)}, u32[]{:S(2)}) collective-permute-start(bf16[64,1024]{1,0:T(8,128)(2,1)S(1)} %get-tuple-element.23), channel_id=1, source_target_pairs={{0,1},{1,0},{2,3},{3,2},{4,5},{5,4},{6,7},{7,6},{8,9},{9,8},{10,11... | collective-permute-start | bytes 393224 | tf_op jit(solution)/shard_map/ppermute | solution.py:323
  82.3 8.3 %collective-permute-start.16 = (bf16[4,2,16,1024]{3,2,1,0:T(8,128)(2,1)S(1)}, bf16[4,2,16,1024]{3,2,1,0:T(8,128)(2,1)S(1)}, u32[]{:S(2)}, u32[]{:S(2)}) collective-permute-start(bf16[4,2,16,1024]{3,2,1,0:T(8,128)(2,1)S(1)} %collective-permute-done.14.refs_6_), channel_id=1, source_target_pairs={{0,56},{8,0},{16,8},{24,16},{32,24},{40,32},{48,40},{56,48},{1,57}... | collective-permute-start | bytes 786440 | tf_op jit(solution)/shard_map/ppermute | solution.py:310
  85.3 8.5 %collective-permute-start.17 = (bf16[4,2,16,1024]{3,2,1,0:T(8,128)(2,1)S(1)}, bf16[4,2,16,1024]{3,2,1,0:T(8,128)(2,1)S(1)}, u32[]{:S(2)}, u32[]{:S(2)}) collective-permute-start(bf16[4,2,16,1024]{3,2,1,0:T(8,128)(2,1)S(1)} %collective-permute-done.15.refs_7_), channel_id=1, source_target_pairs={{0,8},{8,16},{16,24},{24,32},{32,40},{40,48},{48,56},{56,0},{1,9},... | collective-permute-start | bytes 786440 | tf_op jit(solution)/shard_map/ppermute | solution.py:307
  85.3 17.6 %collective-permute-start.6 = (bf16[16,8,16,128]{3,2,1,0:T(8,128)(2,1)S(1)}, bf16[16,8,16,128]{3,2,1,0:T(8,128)(2,1)S(1)}, u32[]{:S(2)}, u32[]{:S(2)}) collective-permute-start(bf16[16,8,16,128]{3,2,1,0:T(8,128)(2,1)S(1)} %slice.21.refs_0_), channel_id=1, source_target_pairs={{0,64},{64,128},{128,192},{192,0},{1,65},{65,129},{129,193},{193,1... | collective-permute-start | bytes 1572872 | tf_op jit(solution)/shard_map/ppermute | solution.py:300
  85.8 17.1 %collective-permute-start.7 = (bf16[16,8,16,128]{3,2,1,0:T(8,128)(2,1)S(1)}, bf16[16,8,16,128]{3,2,1,0:T(8,128)(2,1)S(1)}, u32[]{:S(2)}, u32[]{:S(2)}) collective-permute-start(bf16[16,8,16,128]{3,2,1,0:T(8,128)(2,1)S(1)} %slice.21.refs_0_), channel_id=1, source_target_pairs={{0,192},{64,0},{128,64},{192,128},{1,193},{65,1},{129,65},{193,129... | collective-permute-start | bytes 1572872 | tf_op jit(solution)/shard_map/ppermute | solution.py:300
  88.1 22.2 %collective-permute-start.8 = (bf16[16,8,16,128]{3,2,1,0:T(8,128)(2,1)S(1)}, bf16[16,8,16,128]{3,2,1,0:T(8,128)(2,1)S(1)}, u32[]{:S(2)}, u32[]{:S(2)}) collective-permute-start(bf16[16,8,16,128]{3,2,1,0:T(8,128)(2,1)S(1)} %slice.21.refs_0_), channel_id=1, source_target_pairs={{0,128},{64,192},{128,0},{192,64},{1,129},{65,193},{129,1},{193,65... | collective-permute-start | bytes 1572872 | tf_op jit(solution)/shard_map/ppermute | solution.py:300
  90.7 4.1 %collective-permute-start.4 = (bf16[64,1024]{1,0:T(8,128)(2,1)S(1)}, bf16[64,1024]{1,0:T(8,128)(2,1)S(1)}, u32[]{:S(2)}, u32[]{:S(2)}) collective-permute-start(bf16[64,1024]{1,0:T(8,128)(2,1)S(1)} %add_convert_fusion.7), channel_id=1, source_target_pairs={{0,2},{2,0},{1,3},{3,1},{4,6},{6,4},{5,7},{7,5},{8,10},{10,8},{9,1... | collective-permute-start | bytes 393224 | tf_op jit(solution)/shard_map/ppermute | solution.py:325
  93.8 6.5 %collective-permute-start.18 = (bf16[4,2,16,1024]{3,2,1,0:T(8,128)(2,1)S(1)}, bf16[4,2,16,1024]{3,2,1,0:T(8,128)(2,1)S(1)}, u32[]{:S(2)}, u32[]{:S(2)}) collective-permute-start(bf16[4,2,16,1024]{3,2,1,0:T(8,128)(2,1)S(1)} %collective-permute-done.16.refs_8_), channel_id=1, source_target_pairs={{0,56},{8,0},{16,8},{24,16},{32,24},{40,32},{48,40},{56,48},{1,57}... | collective-permute-start | bytes 786440 | tf_op jit(solution)/shard_map/ppermute | solution.py:310
  94.8 8.1 %collective-permute-start.19 = (bf16[4,2,16,1024]{3,2,1,0:T(8,128)(2,1)S(1)}, bf16[4,2,16,1024]{3,2,1,0:T(8,128)(2,1)S(1)}, u32[]{:S(2)}, u32[]{:S(2)}) collective-permute-start(bf16[4,2,16,1024]{3,2,1,0:T(8,128)(2,1)S(1)} %collective-permute-done.17.refs_9_), channel_id=1, source_target_pairs={{0,8},{8,16},{16,24},{24,32},{32,40},{40,48},{48,56},{56,0},{1,9},... | collective-permute-start | bytes 786440 | tf_op jit(solution)/shard_map/ppermute | solution.py:307
  100.2 10.0 %collective-permute-start.5 = (bf16[64,1024]{1,0:T(8,128)(2,1)S(1)}, bf16[64,1024]{1,0:T(8,128)(2,1)S(1)}, u32[]{:S(2)}, u32[]{:S(2)}) collective-permute-start(bf16[64,1024]{1,0:T(8,128)(2,1)S(1)} %add_convert_fusion.6.mine_ref), channel_id=1, source_target_pairs={{0,1},{1,0},{2,3},{3,2},{4,5},{5,4},{6,7},{7,6},{8,9},{9,8},{10,11... | collective-permute-start | bytes 393224 | tf_op jit(solution)/shard_map/ppermute | solution.py:327
  112.7 3.0 %collective-permute-start.23 = (bf16[64,1024]{1,0:T(8,128)(2,1)S(1)}, bf16[64,1024]{1,0:T(8,128)(2,1)S(1)}, u32[]{:S(2)}, u32[]{:S(2)}) collective-permute-start(bf16[64,1024]{1,0:T(8,128)(2,1)S(1)} %get-tuple-element.27), channel_id=1, source_target_pairs={{0,1},{1,0},{2,3},{3,2},{4,5},{5,4},{6,7},{7,6},{8,9},{9,8},{10,11... | collective-permute-start | bytes 393224 | tf_op jit(solution)/shard_map/ppermute | solution.py:323
  115.8 5.3 %collective-permute-start.24 = (bf16[64,1024]{1,0:T(8,128)(2,1)S(1)}, bf16[64,1024]{1,0:T(8,128)(2,1)S(1)}, u32[]{:S(2)}, u32[]{:S(2)}) collective-permute-start(bf16[64,1024]{1,0:T(8,128)(2,1)S(1)} %add_convert_fusion.5), channel_id=1, source_target_pairs={{0,2},{2,0},{1,3},{3,1},{4,6},{6,4},{5,7},{7,5},{8,10},{10,8},{9,1... | collective-permute-start | bytes 393224 | tf_op jit(solution)/shard_map/ppermute | solution.py:325
  116.3 8.4 %collective-permute-start.20 = (bf16[16,4,16,128]{3,2,1,0:T(8,128)(2,1)S(1)}, bf16[16,4,16,128]{3,2,1,0:T(8,128)(2,1)S(1)}, u32[]{:S(2)}, u32[]{:S(2)}) collective-permute-start(bf16[16,4,16,128]{3,2,1,0:T(8,128)(2,1)S(1)} %get-tuple-element.35.refs_0_), channel_id=1, source_target_pairs={{0,64},{64,128},{128,192},{192,0},{1,65},{65,129},{129,193},{193,1... | collective-permute-start | bytes 786440 | tf_op jit(solution)/shard_map/ppermute | solution.py:300
  116.9 11.5 %collective-permute-start.21 = (bf16[16,4,16,128]{3,2,1,0:T(8,128)(2,1)S(1)}, bf16[16,4,16,128]{3,2,1,0:T(8,128)(2,1)S(1)}, u32[]{:S(2)}, u32[]{:S(2)}) collective-permute-start(bf16[16,4,16,128]{3,2,1,0:T(8,128)(2,1)S(1)} %get-tuple-element.35.refs_0_), channel_id=1, source_target_pairs={{0,192},{64,0},{128,64},{192,128},{1,193},{65,1},{129,65},{193,129... | collective-permute-start | bytes 786440 | tf_op jit(solution)/shard_map/ppermute | solution.py:300
  119.0 12.6 %collective-permute-start.22 = (bf16[16,4,16,128]{3,2,1,0:T(8,128)(2,1)S(1)}, bf16[16,4,16,128]{3,2,1,0:T(8,128)(2,1)S(1)}, u32[]{:S(2)}, u32[]{:S(2)}) collective-permute-start(bf16[16,4,16,128]{3,2,1,0:T(8,128)(2,1)S(1)} %get-tuple-element.35.refs_0_), channel_id=1, source_target_pairs={{0,128},{64,192},{128,0},{192,64},{1,129},{65,193},{129,1},{193,65... | collective-permute-start | bytes 786440 | tf_op jit(solution)/shard_map/ppermute | solution.py:300
  120.2 32.7 %collective-permute-start.29 = (bf16[16,16,16,128]{3,2,1,0:T(8,128)(2,1)S(1)}, bf16[16,16,16,128]{3,2,1,0:T(8,128)(2,1)S(1)}, u32[]{:S(2)}, u32[]{:S(2)}) collective-permute-start(bf16[16,16,16,128]{3,2,1,0:T(8,128)(2,1)S(1)} %all-to-all-done.1.refs_0_), channel_id=1, source_target_pairs={{0,64},{64,128},{128,192},{192,0},{1,65},{65,129},{129,193},{193,1... | collective-permute-start | bytes 3145736 | tf_op jit(solution)/shard_map/ppermute | solution.py:294
  121.0 31.9 %collective-permute-start.30 = (bf16[16,16,16,128]{3,2,1,0:T(8,128)(2,1)S(1)}, bf16[16,16,16,128]{3,2,1,0:T(8,128)(2,1)S(1)}, u32[]{:S(2)}, u32[]{:S(2)}) collective-permute-start(bf16[16,16,16,128]{3,2,1,0:T(8,128)(2,1)S(1)} %all-to-all-done.1.refs_0_), channel_id=1, source_target_pairs={{0,192},{64,0},{128,64},{192,128},{1,193},{65,1},{129,65},{193,129... | collective-permute-start | bytes 3145736 | tf_op jit(solution)/shard_map/ppermute | solution.py:294
  124.7 6.8 %collective-permute-start.25 = (bf16[64,1024]{1,0:T(8,128)(2,1)S(1)}, bf16[64,1024]{1,0:T(8,128)(2,1)S(1)}, u32[]{:S(2)}, u32[]{:S(2)}) collective-permute-start(bf16[64,1024]{1,0:T(8,128)(2,1)S(1)} %add_convert_fusion.4.refs_4_), channel_id=1, source_target_pairs={{0,1},{1,0},{2,3},{3,2},{4,5},{5,4},{6,7},{7,6},{8,9},{9,8},{10,11... | collective-permute-start | bytes 393224 | tf_op jit(solution)/shard_map/ppermute | solution.py:327
  131.6 3.4 %copy-start.1 = (bf16[2,8,256,1024]{3,2,1,0:T(8,128)(2,1)S(1)}, bf16[2,8,256,1024]{3,2,1,0:T(8,128)(2,1)}, u32[]{:S(2)}) copy-start(bf16[2,8,256,1024]{3,2,1,0:T(8,128)(2,1)} %norm_media.1) | copy-start | bytes 25165828
  144.0 36.0 %copy-start.6 = (f32[1024]{0:T(1024)S(1)}, f32[1024]{0:T(1024)}, u32[]{:S(2)}) copy-start(f32[1024]{0:T(1024)} %param.19) | copy-start | bytes 12292
  144.0 11.7 %collective-permute-start.26 = (bf16[64,1024]{1,0:T(8,128)(2,1)S(1)}, bf16[64,1024]{1,0:T(8,128)(2,1)S(1)}, u32[]{:S(2)}, u32[]{:S(2)}) collective-permute-start(bf16[64,1024]{1,0:T(8,128)(2,1)S(1)} %get-tuple-element.30), channel_id=1, source_target_pairs={{0,1},{1,0},{2,3},{3,2},{4,5},{5,4},{6,7},{7,6},{8,9},{9,8},{10,11... | collective-permute-start | bytes 393224 | tf_op jit(solution)/shard_map/ppermute | solution.py:323
  152.9 13.3 %collective-permute-start.31 = (bf16[8,16,16,128]{3,2,1,0:T(8,128)(2,1)S(1)}, bf16[8,16,16,128]{3,2,1,0:T(8,128)(2,1)S(1)}, u32[]{:S(2)}, u32[]{:S(2)}) collective-permute-start(bf16[8,16,16,128]{3,2,1,0:T(8,128)(2,1)S(1)} %slice.23), channel_id=1, source_target_pairs={{0,64},{64,128},{128,192},{192,0},{1,65},{65,129},{129,193},{193,1... | collective-permute-start | bytes 1572872 | tf_op jit(solution)/shard_map/ppermute | solution.py:295
  153.0 13.1 %collective-permute-start.32 = (bf16[8,16,16,128]{3,2,1,0:T(8,128)(2,1)S(1)}, bf16[8,16,16,128]{3,2,1,0:T(8,128)(2,1)S(1)}, u32[]{:S(2)}, u32[]{:S(2)}) collective-permute-start(bf16[8,16,16,128]{3,2,1,0:T(8,128)(2,1)S(1)} %slice.24), channel_id=1, source_target_pairs={{0,192},{64,0},{128,64},{192,128},{1,193},{65,1},{129,65},{193,129... | collective-permute-start | bytes 1572872 | tf_op jit(solution)/shard_map/ppermute | solution.py:295
  155.8 4.2 %collective-permute-start.27 = (bf16[64,1024]{1,0:T(8,128)(2,1)S(1)}, bf16[64,1024]{1,0:T(8,128)(2,1)S(1)}, u32[]{:S(2)}, u32[]{:S(2)}) collective-permute-start(bf16[64,1024]{1,0:T(8,128)(2,1)S(1)} %add_convert_fusion.3), channel_id=1, source_target_pairs={{0,2},{2,0},{1,3},{3,1},{4,6},{6,4},{5,7},{7,5},{8,10},{10,8},{9,1... | collective-permute-start | bytes 393224 | tf_op jit(solution)/shard_map/ppermute | solution.py:325
  160.0 4.0 %collective-permute-start.28 = (bf16[64,1024]{1,0:T(8,128)(2,1)S(1)}, bf16[64,1024]{1,0:T(8,128)(2,1)S(1)}, u32[]{:S(2)}, u32[]{:S(2)}) collective-permute-start(bf16[64,1024]{1,0:T(8,128)(2,1)S(1)} %add_convert_fusion.2.mine_ref), channel_id=1, source_target_pairs={{0,1},{1,0},{2,3},{3,2},{4,5},{5,4},{6,7},{7,6},{8,9},{9,8},{10,11... | collective-permute-start | bytes 393224 | tf_op jit(solution)/shard_map/ppermute | solution.py:327
  168.8 3.4 %collective-permute-start.33 = (bf16[64,1024]{1,0:T(8,128)(2,1)S(1)}, bf16[64,1024]{1,0:T(8,128)(2,1)S(1)}, u32[]{:S(2)}, u32[]{:S(2)}) collective-permute-start(bf16[64,1024]{1,0:T(8,128)(2,1)S(1)} %get-tuple-element.34), channel_id=1, source_target_pairs={{0,1},{1,0},{2,3},{3,2},{4,5},{5,4},{6,7},{7,6},{8,9},{9,8},{10,11... | collective-permute-start | bytes 393224 | tf_op jit(solution)/shard_map/ppermute | solution.py:323
  172.3 4.8 %collective-permute-start.34 = (bf16[64,1024]{1,0:T(8,128)(2,1)S(1)}, bf16[64,1024]{1,0:T(8,128)(2,1)S(1)}, u32[]{:S(2)}, u32[]{:S(2)}) collective-permute-start(bf16[64,1024]{1,0:T(8,128)(2,1)S(1)} %add_convert_fusion.1), channel_id=1, source_target_pairs={{0,2},{2,0},{1,3},{3,1},{4,6},{6,4},{5,7},{7,5},{8,10},{10,8},{9,1... | collective-permute-start | bytes 393224 | tf_op jit(solution)/shard_map/ppermute | solution.py:325
  177.1 2.3 %collective-permute-start.35 = (bf16[64,1024]{1,0:T(8,128)(2,1)S(1)}, bf16[64,1024]{1,0:T(8,128)(2,1)S(1)}, u32[]{:S(2)}, u32[]{:S(2)}) collective-permute-start(bf16[64,1024]{1,0:T(8,128)(2,1)S(1)} %add_convert_fusion), channel_id=1, source_target_pairs={{0,1},{1,0},{2,3},{3,2},{4,5},{5,4},{6,7},{7,6},{8,9},{9,8},{10,11... | collective-permute-start | bytes 393224 | tf_op jit(solution)/shard_map/ppermute | solution.py:327
where the time goes:
time: 181 us
  starting transfers between devices  73.8 us (41%)
  waiting for transfers between devices  59.5 us (33%)
  Pallas kernels  37.7 us (21%)
  local copies, waits for them, and re-layouts  7.09 us (4%)
  other arithmetic  2.47 us (1%)
    pallas_call x2, Pallas kernels, attention(): pl.pallas_call(functools.partial(attention_kernel, layer), in_specs=[pl.B...  18 us
    ppermute x12, waiting for transfers between devices, x_direct(): lax.ppermute(own, 'x', ring_pairs(4, step))  15.5 us
    ppermute x12, starting transfers between devices, x_direct(): lax.ppermute(own, 'x', ring_pairs(4, step))  15.5 us
    all_to_all x1, waiting for transfers between devices, on_device(): first = lax.all_to_all(first, ('z', 'yh'), 0, 0, tiled=True)  12.3 us
    pallas_call x1, Pallas kernels, norm_media(): pl.pallas_call(media_kernel, in_specs=[anywhere, pl.BlockSpec(memory_spac...  11.8 us
    all_to_all x1, starting transfers between devices, on_device(): first = lax.all_to_all(first, ('z', 'yh'), 0, 0, tiled=True)  11.8 us
    ppermute x4, starting transfers between devices, total(): got = lax.ppermute(give, 'c', swap)  10.4 us
    ppermute x4, starting transfers between devices, total(): return (full, lax.ppermute(full, 'c', swap))  10.2 us
  transfers between devices with their start and end apart: 38, of which 20 were waited for; matrix products, arithmetic and copies ran while one was open for 1% of the time, Pallas kernels for 18%

commit v1 on v0

--- a/solution.py
+++ b/solution.py
@@ -9,7 +9,7 @@
 
 HEAD = 64
 LAYERS = 2
-CHUNK = 512
+CHUNK = 2048
 F32, BF16 = jnp.float32, jnp.bfloat16
 DP = ("x", "z", "yh")
 MP = ("yl", "c")
@@ -230,7 +230,7 @@
             pltpu.VMEM((s, t + lat, 2 * lat), F32),
             pltpu.VMEM((s, t + lat, 128), BF16),
         ],
-        compiler_params=params(24),
+        compiler_params=params(16),
         cost_estimate=pl.CostEstimate(flops=6 * 10**9, bytes_accessed=10 * 2**20, transcendentals=10**6),
         name="attention",
     )(places, media_normed, state, gain, media_gain, *pieces, *update)
@@ -282,7 +282,7 @@
             pltpu.VMEM((d // 16, 16, 1024), BF16),
             pltpu.VMEM((rows, d), BF16),
         ],
-        compiler_params=params(24),
+        compiler_params=params(14),
         cost_estimate=pl.CostEstimate(flops=2 * 10**9, bytes_accessed=5 * 2**20, transcendentals=10**5),
         name="ffn",
     )(places, state, *update, gain, *pieces)

time: 181 us -> 179 us (0.989)
  Pallas kernels: 37.7 us -> 33.7 us
  waiting for transfers between devices: 59.5 us -> 61.5 us
    pallas_call x2, Pallas kernels: 18 us -> 14 us  [attention(): pl.pallas_call(functools.partial(attention_kernel, layer), in_specs=[pl.B...]
    ppermute x2, waiting for transfers between devices: 6.15 us -> 8.16 us  [x_ring(): a, b = (lax.ppermute(own, 'x', right), lax.ppermute(own, 'x', left))]
  transfers between devices with their start and end apart: 38 -> 38, of which waited for: 20 -> 20; matrix products, arithmetic and copies ran while one was open for 1% -> 1% of each run, Pallas kernels for 18% -> 16%
where the time goes in v1:
time: 179 us
  starting transfers between devices  73.8 us (41%)
  waiting for transfers between devices  61.5 us (34%)
  Pallas kernels  33.7 us (19%)
  local copies, waits for them, and re-layouts  7.09 us (4%)
  other arithmetic  2.46 us (1%)
    ppermute x12, waiting for transfers between devices, x_direct(): lax.ppermute(own, 'x', ring_pairs(4, step))  15.5 us
    ppermute x12, starting transfers between devices, x_direct(): lax.ppermute(own, 'x', ring_pairs(4, step))  15.5 us
    pallas_call x2, Pallas kernels, attention(): pl.pallas_call(functools.partial(attention_kernel, layer), in_specs=[pl.B...  14 us
    all_to_all x1, waiting for transfers between devices, on_device(): first = lax.all_to_all(first, ('z', 'yh'), 0, 0, tiled=True)  12.3 us
    pallas_call x1, Pallas kernels, norm_media(): pl.pallas_call(media_kernel, in_specs=[anywhere, pl.BlockSpec(memory_spac...  11.8 us
    all_to_all x1, starting transfers between devices, on_device(): first = lax.all_to_all(first, ('z', 'yh'), 0, 0, tiled=True)  11.8 us
    ppermute x4, starting transfers between devices, total(): got = lax.ppermute(give, 'c', swap)  10.4 us
    ppermute x4, starting transfers between devices, total(): return (full, lax.ppermute(full, 'c', swap))  10.2 us
  transfers between devices with their start and end apart: 38, of which 20 were waited for; matrix products, arithmetic and copies ran while one was open for 1% of the time, Pallas kernels for 16%

profile of v1, /device:TPU:1, one launch (start us, length us, event | category | flops | bytes accessed | tf_op | source)
XLA Modules:
  0.0 178.9 jit_solution(16115794257266596091)
XLA Ops:
  0.0 2.9 %pack.1 = (bf16[16,16,16,128]{3,2,1,0:T(8,128)(2,1)}, bf16[16,16,16,128]{3,2,1,0:T(8,128)(2,1)}, bf16[16,1024]{1,0:T(8,128)(2,1)}) custom-call(bf16[2,16,128]{2,1,0:T(8,128)(2,1)} %q_ref.1, bf16[2,16,128]{2,1,0:T(8,128)(2,1)} %k_ref.1, bf16[2,16,128]{2,1,0:T(8,128)(2,1)} %v_ref.1, bf16[2,16,128]{2,1,0:T(8,128)(2,1)} %bitcast.40, bf16[2,16,1024]{2,1,0:T(8,128)(2,1)} %u_ref.1, ...), custom_call_target="tpu_custom_call" | custom-call | tf_op jit(solution)/shard_map/pack/pallas_call | solution.py:61
  2.9 11.8 %all-to-all-start = ((bf16[16,16,16,128]{3,2,1,0:T(8,128)(2,1)}), bf16[16,16,16,128]{3,2,1,0:T(8,128)(2,1)S(1)}, u32[]{:S(2)}, u32[]{:S(2)}) async-start(bf16[16,16,16,128]{3,2,1,0:T(8,128)(2,1)} %get-tuple-element.20), calls=%async_computation | async-start | bytes 2097152 | tf_op jit(solution)/shard_map/all_to_all | solution.py:340
  14.7 2.9 %collective-permute-start.9 = (bf16[16,1024]{1,0:T(8,128)(2,1)}, bf16[16,1024]{1,0:T(8,128)(2,1)S(1)}, u32[]{:S(2)}, u32[]{:S(2)}) collective-permute-start(bf16[16,1024]{1,0:T(8,128)(2,1)} %get-tuple-element.24), channel_id=1, source_target_pairs={{0,4},{4,0},{1,5},{5,1},{2,6},{6,2},{3,7},{7,3},{8,12},{12,8},{9,1... | collective-permute-start | bytes 98312 | tf_op jit(solution)/shard_map/ppermute | solution.py:316
  17.5 2.2 %collective-permute-done.9 = bf16[16,1024]{1,0:T(8,128)(2,1)S(1)} collective-permute-done((bf16[16,1024]{1,0:T(8,128)(2,1)}, bf16[16,1024]{1,0:T(8,128)(2,1)S(1)}, u32[]{:S(2)}, u32[]{:S(2)}) %collective-permute-start.9) | collective-permute-done | bytes 32800 | tf_op jit(solution)/shard_map/ppermute | solution.py:316
  19.7 0.8 fusion.1
  20.5 1.3 collective-permute-start.10
  21.8 1.5 collective-permute-start.11
  23.3 1.5 collective-permute-start.12
  24.9 0.3 collective-permute-done.10
  25.2 3.1 %collective-permute-done.12 = bf16[2,16,1024]{2,1,0:T(8,128)(2,1)S(1)} collective-permute-done((bf16[2,16,1024]{2,1,0:T(8,128)(2,1)S(1)}, bf16[2,16,1024]{2,1,0:T(8,128)(2,1)S(1)}, u32[]{:S(2)}, u32[]{:S(2)}) %collective-permute-start.12) | collective-permute-done | bytes 65568 | tf_op jit(solution)/shard_map/ppermute | solution.py:300
  28.3 1.0 collective-permute-start.13
  29.3 12.3 %all-to-all-done = bf16[16,16,16,128]{3,2,1,0:T(8,128)(2,1)S(1)} async-done(((bf16[16,16,16,128]{3,2,1,0:T(8,128)(2,1)}), bf16[16,16,16,128]{3,2,1,0:T(8,128)(2,1)S(1)}, u32[]{:S(2)}, u32[]{:S(2)}) %all-to-all-start) | async-done | bytes 1048608 | tf_op jit(solution)/shard_map/all_to_all | solution.py:340
  41.6 6.2 %all-to-all-start.1 = ((bf16[16,16,16,128]{3,2,1,0:T(8,128)(2,1)}), bf16[16,16,16,128]{3,2,1,0:T(8,128)(2,1)S(1)}, u32[]{:S(2)}, u32[]{:S(2)}) async-start(bf16[16,16,16,128]{3,2,1,0:T(8,128)(2,1)} %get-tuple-element.31), calls=%async_computation.1 | async-start | bytes 2097152 | tf_op jit(solution)/shard_map/all_to_all | solution.py:343
  47.9 1.3 collective-permute-start
  49.2 1.5 collective-permute-start.1
  50.7 1.5 collective-permute-start.2
  52.2 11.8 %norm_media.1 = bf16[2,8,256,1024]{3,2,1,0:T(8,128)(2,1)} custom-call(bf16[2,8,256,1024]{3,2,1,0:T(8,128)(2,1)} %m_ref.1, bf16[8,1024]{1,0:T(8,128)(2,1)} %t_ref.1), custom_call_target="tpu_custom_call" | custom-call | flops 3000000000 | bytes 16777216 | tf_op jit(solution)/shard_map/norm_media/pallas_call | solution.py:136
  64.0 2.7 %collective-permute-start.14 = (bf16[4,2,16,1024]{3,2,1,0:T(8,128)(2,1)S(1)}, bf16[4,2,16,1024]{3,2,1,0:T(8,128)(2,1)S(1)}, u32[]{:S(2)}, u32[]{:S(2)}) collective-permute-start(bf16[4,2,16,1024]{3,2,1,0:T(8,128)(2,1)S(1)} %pad_maximum_fusion.refs_4_), channel_id=1, source_target_pairs={{0,56},{8,0},{16,8},{24,16},{32,24},{40,32},{48,40},{56,48},{1,57}... | collective-permute-start | bytes 786440 | tf_op jit(solution)/shard_map/ppermute | solution.py:310
  66.7 3.4 %copy-done = bf16[2,8,256,1024]{3,2,1,0:T(8,128)(2,1)S(1)} copy-done((bf16[2,8,256,1024]{3,2,1,0:T(8,128)(2,1)S(1)}, bf16[2,8,256,1024]{3,2,1,0:T(8,128)(2,1)}, u32[]{:S(2)}) %copy-start) | copy-done | bytes 8388632
  70.1 7.0 %attention.2 = (bf16[64,1024]{1,0:T(8,128)(2,1)S(1)}, bf16[64,1024]{1,0:T(8,128)(2,1)S(1)}, f32[2,64,1024]{2,1,0:T(8,128)S(1)}) custom-call(s32[4]{0:T(128)S(1)} %pad_add_fusion.at_ref, bf16[2,2048,1024]{2,1,0:T(8,128)(2,1)S(1)} %bitcast.28, bf16[64,1024]{1,0:T(8,128)(2,1)S(1)} %copy-done.2, f32[2,1024]{1,0:T(2,128)S(1)} %copy-done.3, ...), custom_call_target="tpu_custom_call" | custom-call | flops 6000000000 | bytes 10485760 | tf_op jit(solution)/shard_map/attention/pallas_call | solution.py:222
  77.0 3.3 %collective-permute-start.3 = (bf16[64,1024]{1,0:T(8,128)(2,1)S(1)}, bf16[64,1024]{1,0:T(8,128)(2,1)S(1)}, u32[]{:S(2)}, u32[]{:S(2)}) collective-permute-start(bf16[64,1024]{1,0:T(8,128)(2,1)S(1)} %get-tuple-element.23), channel_id=1, source_target_pairs={{0,1},{1,0},{2,3},{3,2},{4,5},{5,4},{6,7},{7,6},{8,9},{9,8},{10,11... | collective-permute-start | bytes 393224 | tf_op jit(solution)/shard_map/ppermute | solution.py:323
  80.3 2.9 %collective-permute-start.16 = (bf16[4,2,16,1024]{3,2,1,0:T(8,128)(2,1)S(1)}, bf16[4,2,16,1024]{3,2,1,0:T(8,128)(2,1)S(1)}, u32[]{:S(2)}, u32[]{:S(2)}) collective-permute-start(bf16[4,2,16,1024]{3,2,1,0:T(8,128)(2,1)S(1)} %collective-permute-done.14.refs_6_), channel_id=1, source_target_pairs={{0,56},{8,0},{16,8},{24,16},{32,24},{40,32},{48,40},{56,48},{1,57}... | collective-permute-start | bytes 786440 | tf_op jit(solution)/shard_map/ppermute | solution.py:310
  83.3 0.4 collective-permute-start.6
  83.7 2.3 %collective-permute-start.7 = (bf16[16,8,16,128]{3,2,1,0:T(8,128)(2,1)S(1)}, bf16[16,8,16,128]{3,2,1,0:T(8,128)(2,1)S(1)}, u32[]{:S(2)}, u32[]{:S(2)}) collective-permute-start(bf16[16,8,16,128]{3,2,1,0:T(8,128)(2,1)S(1)} %slice.21.refs_0_), channel_id=1, source_target_pairs={{0,192},{64,0},{128,64},{192,128},{1,193},{65,1},{129,65},{193,129... | collective-permute-start | bytes 1572872 | tf_op jit(solution)/shard_map/ppermute | solution.py:300
  86.1 0.3 collective-permute-start.8
  86.4 2.3 %collective-permute-done.16.refs_8_ = bf16[4,2,16,1024]{3,2,1,0:T(8,128)(2,1)S(1)} collective-permute-done((bf16[4,2,16,1024]{3,2,1,0:T(8,128)(2,1)S(1)}, bf16[4,2,16,1024]{3,2,1,0:T(8,128)(2,1)S(1)}, u32[]{:S(2)}, u32[]{:S(2)}) %collective-permute-start.16) | collective-permute-done | bytes 262176 | tf_op jit(solution)/shard_map/ppermute | solution.py:310
  88.6 0.4 collective-permute-start.4
  89.1 2.7 %collective-permute-done.17.refs_9_ = bf16[4,2,16,1024]{3,2,1,0:T(8,128)(2,1)S(1)} collective-permute-done((bf16[4,2,16,1024]{3,2,1,0:T(8,128)(2,1)S(1)}, bf16[4,2,16,1024]{3,2,1,0:T(8,128)(2,1)S(1)}, u32[]{:S(2)}, u32[]{:S(2)}) %collective-permute-start.17) | collective-permute-done | bytes 262176 | tf_op jit(solution)/shard_map/ppermute | solution.py:307
  91.8 0.7 collective-permute-start.18
  92.7 0.5 collective-permute-start.19
  93.3 4.9 %collective-permute-done.18.refs_10_ = bf16[4,2,16,1024]{3,2,1,0:T(8,128)(2,1)S(1)} collective-permute-done((bf16[4,2,16,1024]{3,2,1,0:T(8,128)(2,1)S(1)}, bf16[4,2,16,1024]{3,2,1,0:T(8,128)(2,1)S(1)}, u32[]{:S(2)}, u32[]{:S(2)}) %collective-permute-start.18) | collective-permute-done | bytes 262176 | tf_op jit(solution)/shard_map/ppermute | solution.py:310
  98.2 2.3 %collective-permute-start.5 = (bf16[64,1024]{1,0:T(8,128)(2,1)S(1)}, bf16[64,1024]{1,0:T(8,128)(2,1)S(1)}, u32[]{:S(2)}, u32[]{:S(2)}) collective-permute-start(bf16[64,1024]{1,0:T(8,128)(2,1)S(1)} %add_convert_fusion.6.mine_ref), channel_id=1, source_target_pairs={{0,1},{1,0},{2,3},{3,2},{4,5},{5,4},{6,7},{7,6},{8,9},{9,8},{10,11... | collective-permute-start | bytes 393224 | tf_op jit(solution)/shard_map/ppermute | solution.py:327
  100.5 0.4 collective-permute-done.19.refs_11_
  100.9 7.4 %collective-permute-done.8.refs_3_ = bf16[16,8,16,128]{3,2,1,0:T(8,128)(2,1)S(1)} collective-permute-done((bf16[16,8,16,128]{3,2,1,0:T(8,128)(2,1)S(1)}, bf16[16,8,16,128]{3,2,1,0:T(8,128)(2,1)S(1)}, u32[]{:S(2)}, u32[]{:S(2)}) %collective-permute-start.8) | collective-permute-done | bytes 524320 | tf_op jit(solution)/shard_map/ppermute | solution.py:300
  108.2 2.4 %ffn.2 = (bf16[64,1024]{1,0:T(8,128)(2,1)S(1)}, bf16[64,1024]{1,0:T(8,128)(2,1)S(1)}, f32[128,1024]{1,0:T(8,128)S(1)}) custom-call(s32[4]{0:T(128)S(1)} %pad_add_fusion.at_ref, f32[128,1024]{1,0:T(8,128)S(1)} %bitcast.31, bf16[64,1024]{1,0:T(8,128)(2,1)S(1)} %add_convert_fusion.6.mine_ref, bf16[64,1024]{1,0:T(8,128)(2,1)S(1)} %collective-permute-done.5.theirs_ref, ...), custom_call_target="tpu_custom_call" | custom-call | flops 2000000000 | bytes 5242880 | tf_op jit(solution)/shard_map/ffn/pallas_call | solution.py:275
  110.7 2.1 %collective-permute-start.23 = (bf16[64,1024]{1,0:T(8,128)(2,1)S(1)}, bf16[64,1024]{1,0:T(8,128)(2,1)S(1)}, u32[]{:S(2)}, u32[]{:S(2)}) collective-permute-start(bf16[64,1024]{1,0:T(8,128)(2,1)S(1)} %get-tuple-element.27), channel_id=1, source_target_pairs={{0,1},{1,0},{2,3},{3,2},{4,5},{5,4},{6,7},{7,6},{8,9},{9,8},{10,11... | collective-permute-start | bytes 393224 | tf_op jit(solution)/shard_map/ppermute | solution.py:323
  112.7 1.0 collective-permute-done.23
  113.7 0.5 collective-permute-start.24
  114.3 0.6 collective-permute-start.20
  114.8 2.1 %collective-permute-start.21 = (bf16[16,4,16,128]{3,2,1,0:T(8,128)(2,1)S(1)}, bf16[16,4,16,128]{3,2,1,0:T(8,128)(2,1)S(1)}, u32[]{:S(2)}, u32[]{:S(2)}) collective-permute-start(bf16[16,4,16,128]{3,2,1,0:T(8,128)(2,1)S(1)} %get-tuple-element.35.refs_0_), channel_id=1, source_target_pairs={{0,192},{64,0},{128,64},{192,128},{1,193},{65,1},{129,65},{193,129... | collective-permute-start | bytes 786440 | tf_op jit(solution)/shard_map/ppermute | solution.py:300
  117.0 1.2 collective-permute-start.22
  118.1 0.9 collective-permute-start.29
  119.0 2.2 %collective-permute-start.30 = (bf16[16,16,16,128]{3,2,1,0:T(8,128)(2,1)S(1)}, bf16[16,16,16,128]{3,2,1,0:T(8,128)(2,1)S(1)}, u32[]{:S(2)}, u32[]{:S(2)}) collective-permute-start(bf16[16,16,16,128]{3,2,1,0:T(8,128)(2,1)S(1)} %all-to-all-done.1.refs_0_), channel_id=1, source_target_pairs={{0,192},{64,0},{128,64},{192,128},{1,193},{65,1},{129,65},{193,129... | collective-permute-start | bytes 3145736 | tf_op jit(solution)/shard_map/ppermute | solution.py:294
  121.2 1.5 collective-permute-done.20.refs_1_
  122.7 3.6 %collective-permute-start.25 = (bf16[64,1024]{1,0:T(8,128)(2,1)S(1)}, bf16[64,1024]{1,0:T(8,128)(2,1)S(1)}, u32[]{:S(2)}, u32[]{:S(2)}) collective-permute-start(bf16[64,1024]{1,0:T(8,128)(2,1)S(1)} %add_convert_fusion.4.refs_4_), channel_id=1, source_target_pairs={{0,1},{1,0},{2,3},{3,2},{4,5},{5,4},{6,7},{7,6},{8,9},{9,8},{10,11... | collective-permute-start | bytes 393224 | tf_op jit(solution)/shard_map/ppermute | solution.py:327
  126.3 3.2 %collective-permute-done.22.refs_3_ = bf16[16,4,16,128]{3,2,1,0:T(8,128)(2,1)S(1)} collective-permute-done((bf16[16,4,16,128]{3,2,1,0:T(8,128)(2,1)S(1)}, bf16[16,4,16,128]{3,2,1,0:T(8,128)(2,1)S(1)}, u32[]{:S(2)}, u32[]{:S(2)}) %collective-permute-start.22) | collective-permute-done | bytes 262176 | tf_op jit(solution)/shard_map/ppermute | solution.py:300
  129.6 3.4 %copy-done.1 = bf16[2,8,256,1024]{3,2,1,0:T(8,128)(2,1)S(1)} copy-done((bf16[2,8,256,1024]{3,2,1,0:T(8,128)(2,1)S(1)}, bf16[2,8,256,1024]{3,2,1,0:T(8,128)(2,1)}, u32[]{:S(2)}) %copy-start.1) | copy-done | bytes 8388632
  132.9 7.0 %attention.3 = (bf16[64,1024]{1,0:T(8,128)(2,1)S(1)}, bf16[64,1024]{1,0:T(8,128)(2,1)S(1)}, f32[2,64,1024]{2,1,0:T(8,128)S(1)}) custom-call(s32[4]{0:T(128)S(1)} %pad_add_fusion.at_ref, bf16[2,2048,1024]{2,1,0:T(8,128)(2,1)S(1)} %bitcast.29, f32[2,64,1024]{2,1,0:T(8,128)S(1)} %bitcast.32, f32[2,1024]{1,0:T(2,128)S(1)} %copy-done.3, f32[2,1024]{1,0:T(2,128)S(1)} %copy-done.4, ...), custom_call_target="tpu_custom_call" | custom-call | flops 6000000000 | bytes 10485760 | tf_op jit(solution)/shard_map/attention/pallas_call | solution.py:222
  140.0 2.7 %collective-permute-start.26 = (bf16[64,1024]{1,0:T(8,128)(2,1)S(1)}, bf16[64,1024]{1,0:T(8,128)(2,1)S(1)}, u32[]{:S(2)}, u32[]{:S(2)}) collective-permute-start(bf16[64,1024]{1,0:T(8,128)(2,1)S(1)} %get-tuple-element.30), channel_id=1, source_target_pairs={{0,1},{1,0},{2,3},{3,2},{4,5},{5,4},{6,7},{7,6},{8,9},{9,8},{10,11... | collective-permute-start | bytes 393224 | tf_op jit(solution)/shard_map/ppermute | solution.py:323
  142.6 8.2 %collective-permute-done.29.refs_1_ = bf16[16,16,16,128]{3,2,1,0:T(8,128)(2,1)S(1)} collective-permute-done((bf16[16,16,16,128]{3,2,1,0:T(8,128)(2,1)S(1)}, bf16[16,16,16,128]{3,2,1,0:T(8,128)(2,1)S(1)}, u32[]{:S(2)}, u32[]{:S(2)}) %collective-permute-start.29) | collective-permute-done | bytes 1048608 | tf_op jit(solution)/shard_map/ppermute | solution.py:294
  151.0 2.7 %collective-permute-start.32 = (bf16[8,16,16,128]{3,2,1,0:T(8,128)(2,1)S(1)}, bf16[8,16,16,128]{3,2,1,0:T(8,128)(2,1)S(1)}, u32[]{:S(2)}, u32[]{:S(2)}) collective-permute-start(bf16[8,16,16,128]{3,2,1,0:T(8,128)(2,1)S(1)} %slice.24), channel_id=1, source_target_pairs={{0,192},{64,0},{128,64},{192,128},{1,193},{65,1},{129,65},{193,129... | collective-permute-start | bytes 1572872 | tf_op jit(solution)/shard_map/ppermute | solution.py:295
  153.8 1.1 collective-permute-start.27
  154.9 3.1 %collective-permute-done.27 = bf16[64,1024]{1,0:T(8,128)(2,1)S(1)} collective-permute-done((bf16[64,1024]{1,0:T(8,128)(2,1)S(1)}, bf16[64,1024]{1,0:T(8,128)(2,1)S(1)}, u32[]{:S(2)}, u32[]{:S(2)}) %collective-permute-start.27) | collective-permute-done | bytes 131104 | tf_op jit(solution)/shard_map/ppermute | solution.py:325
  158.0 3.0 %collective-permute-start.28 = (bf16[64,1024]{1,0:T(8,128)(2,1)S(1)}, bf16[64,1024]{1,0:T(8,128)(2,1)S(1)}, u32[]{:S(2)}, u32[]{:S(2)}) collective-permute-start(bf16[64,1024]{1,0:T(8,128)(2,1)S(1)} %add_convert_fusion.2.mine_ref), channel_id=1, source_target_pairs={{0,1},{1,0},{2,3},{3,2},{4,5},{5,4},{6,7},{7,6},{8,9},{9,8},{10,11... | collective-permute-start | bytes 393224 | tf_op jit(solution)/shard_map/ppermute | solution.py:327
  161.0 1.0 collective-permute-done.28.theirs_ref
  162.0 2.1 %collective-permute-done.31.refs_3_ = bf16[8,16,16,128]{3,2,1,0:T(8,128)(2,1)S(1)} collective-permute-done((bf16[8,16,16,128]{3,2,1,0:T(8,128)(2,1)S(1)}, bf16[8,16,16,128]{3,2,1,0:T(8,128)(2,1)S(1)}, u32[]{:S(2)}, u32[]{:S(2)}) %collective-permute-start.31) | collective-permute-done | bytes 524320 | tf_op jit(solution)/shard_map/ppermute | solution.py:295
  164.1 2.7 %ffn.3 = (bf16[64,1024]{1,0:T(8,128)(2,1)S(1)}, bf16[64,1024]{1,0:T(8,128)(2,1)S(1)}, f32[128,1024]{1,0:T(8,128)S(1)}) custom-call(s32[4]{0:T(128)S(1)} %pad_add_fusion.at_ref, f32[128,1024]{1,0:T(8,128)S(1)} %bitcast.33, bf16[64,1024]{1,0:T(8,128)(2,1)S(1)} %add_convert_fusion.2.mine_ref, bf16[64,1024]{1,0:T(8,128)(2,1)S(1)} %collective-permute-done.28.theirs_ref, ...), custom_call_target="tpu_custom_call" | custom-call | flops 2000000000 | bytes 5242880 | tf_op jit(solution)/shard_map/ffn/pallas_call | solution.py:275
  166.8 2.4 %collective-permute-start.33 = (bf16[64,1024]{1,0:T(8,128)(2,1)S(1)}, bf16[64,1024]{1,0:T(8,128)(2,1)S(1)}, u32[]{:S(2)}, u32[]{:S(2)}) collective-permute-start(bf16[64,1024]{1,0:T(8,128)(2,1)S(1)} %get-tuple-element.34), channel_id=1, source_target_pairs={{0,1},{1,0},{2,3},{3,2},{4,5},{5,4},{6,7},{7,6},{8,9},{9,8},{10,11... | collective-permute-start | bytes 393224 | tf_op jit(solution)/shard_map/ppermute | solution.py:323
  169.2 1.0 collective-permute-done.33
  170.2 1.1 collective-permute-start.34
  171.4 3.7 %collective-permute-done.34 = bf16[64,1024]{1,0:T(8,128)(2,1)S(1)} collective-permute-done((bf16[64,1024]{1,0:T(8,128)(2,1)S(1)}, bf16[64,1024]{1,0:T(8,128)(2,1)S(1)}, u32[]{:S(2)}, u32[]{:S(2)}) %collective-permute-start.34) | collective-permute-done | bytes 131104 | tf_op jit(solution)/shard_map/ppermute | solution.py:325
  175.1 1.3 collective-permute-start.35
  176.4 1.0 collective-permute-done.35
  178.0 0.9 multiply_convert_fusion
  (56 shorter events, 1.6 us)
Async XLA Ops:
  2.9 38.7 %all-to-all-start = ((bf16[16,16,16,128]{3,2,1,0:T(8,128)(2,1)}), bf16[16,16,16,128]{3,2,1,0:T(8,128)(2,1)S(1)}, u32[]{:S(2)}, u32[]{:S(2)}) async-start(bf16[16,16,16,128]{3,2,1,0:T(8,128)(2,1)} %get-tuple-element.20), calls=%async_computation | async-start | bytes 2097152 | tf_op jit(solution)/shard_map/all_to_all | solution.py:340
  14.7 5.1 %collective-permute-start.9 = (bf16[16,1024]{1,0:T(8,128)(2,1)}, bf16[16,1024]{1,0:T(8,128)(2,1)S(1)}, u32[]{:S(2)}, u32[]{:S(2)}) collective-permute-start(bf16[16,1024]{1,0:T(8,128)(2,1)} %get-tuple-element.24), channel_id=1, source_target_pairs={{0,4},{4,0},{1,5},{5,1},{2,6},{6,2},{3,7},{7,3},{8,12},{12,8},{9,1... | collective-permute-start | bytes 98312 | tf_op jit(solution)/shard_map/ppermute | solution.py:316
  20.5 4.7 %collective-permute-start.10 = (bf16[2,16,1024]{2,1,0:T(8,128)(2,1)S(1)}, bf16[2,16,1024]{2,1,0:T(8,128)(2,1)S(1)}, u32[]{:S(2)}, u32[]{:S(2)}) collective-permute-start(bf16[2,16,1024]{2,1,0:T(8,128)(2,1)S(1)} %get-tuple-element.40), channel_id=1, source_target_pairs={{0,64},{64,128},{128,192},{192,0},{1,65},{65,129},{129,193},{193,1... | collective-permute-start | bytes 196616 | tf_op jit(solution)/shard_map/ppermute | solution.py:300
  21.8 3.4 %collective-permute-start.11 = (bf16[2,16,1024]{2,1,0:T(8,128)(2,1)S(1)}, bf16[2,16,1024]{2,1,0:T(8,128)(2,1)S(1)}, u32[]{:S(2)}, u32[]{:S(2)}) collective-permute-start(bf16[2,16,1024]{2,1,0:T(8,128)(2,1)S(1)} %get-tuple-element.40), channel_id=1, source_target_pairs={{0,192},{64,0},{128,64},{192,128},{1,193},{65,1},{129,65},{193,129... | collective-permute-start | bytes 196616 | tf_op jit(solution)/shard_map/ppermute | solution.py:300
  23.3 5.0 %collective-permute-start.12 = (bf16[2,16,1024]{2,1,0:T(8,128)(2,1)S(1)}, bf16[2,16,1024]{2,1,0:T(8,128)(2,1)S(1)}, u32[]{:S(2)}, u32[]{:S(2)}) collective-permute-start(bf16[2,16,1024]{2,1,0:T(8,128)(2,1)S(1)} %get-tuple-element.40), channel_id=1, source_target_pairs={{0,128},{64,192},{128,0},{192,64},{1,129},{65,193},{129,1},{193,65... | collective-permute-start | bytes 196616 | tf_op jit(solution)/shard_map/ppermute | solution.py:300
  28.3 38.3 %collective-permute-start.13 = (bf16[4,2,16,1024]{3,2,1,0:T(8,128)(2,1)S(1)}, bf16[4,2,16,1024]{3,2,1,0:T(8,128)(2,1)S(1)}, u32[]{:S(2)}, u32[]{:S(2)}) collective-permute-start(bf16[4,2,16,1024]{3,2,1,0:T(8,128)(2,1)S(1)} %pad_maximum_fusion.refs_4_), channel_id=1, source_target_pairs={{0,8},{8,16},{16,24},{24,32},{32,40},{40,48},{48,56},{56,0},{1,9},... | collective-permute-start | bytes 786440 | tf_op jit(solution)/shard_map/ppermute | solution.py:307
  41.6 76.6 %all-to-all-start.1 = ((bf16[16,16,16,128]{3,2,1,0:T(8,128)(2,1)}), bf16[16,16,16,128]{3,2,1,0:T(8,128)(2,1)S(1)}, u32[]{:S(2)}, u32[]{:S(2)}) async-start(bf16[16,16,16,128]{3,2,1,0:T(8,128)(2,1)} %get-tuple-element.31), calls=%async_computation.1 | async-start | bytes 2097152 | tf_op jit(solution)/shard_map/all_to_all | solution.py:343
  47.9 18.8 %copy-start.2 = (bf16[64,1024]{1,0:T(8,128)(2,1)S(1)}, bf16[64,1024]{1,0:T(8,128)(2,1)}, u32[]{:S(2)}) copy-start(bf16[64,1024]{1,0:T(8,128)(2,1)} %s_ref.1) | copy-start | bytes 393220
  47.9 18.8 %copy-start.3 = (f32[2,1024]{1,0:T(2,128)S(1)}, f32[2,1024]{1,0:T(2,128)}, u32[]{:S(2)}) copy-start(f32[2,1024]{1,0:T(2,128)} %g_ref.6) | copy-start | bytes 24580
  47.9 18.8 %copy-start.4 = (f32[2,1024]{1,0:T(2,128)S(1)}, f32[2,1024]{1,0:T(2,128)}, u32[]{:S(2)}) copy-start(f32[2,1024]{1,0:T(2,128)} %mg_ref.3) | copy-start | bytes 24580
  47.9 18.7 %collective-permute-start = (bf16[16,4,16,128]{3,2,1,0:T(8,128)(2,1)S(1)}, bf16[16,4,16,128]{3,2,1,0:T(8,128)(2,1)S(1)}, u32[]{:S(2)}, u32[]{:S(2)}) collective-permute-start(bf16[16,4,16,128]{3,2,1,0:T(8,128)(2,1)S(1)} %get-tuple-element.36.refs_0_), channel_id=1, source_target_pairs={{0,64},{64,128},{128,192},{192,0},{1,65},{65,129},{129,193},{193,1... | collective-permute-start | bytes 786440 | tf_op jit(solution)/shard_map/ppermute | solution.py:300
  49.2 17.4 %collective-permute-start.1 = (bf16[16,4,16,128]{3,2,1,0:T(8,128)(2,1)S(1)}, bf16[16,4,16,128]{3,2,1,0:T(8,128)(2,1)S(1)}, u32[]{:S(2)}, u32[]{:S(2)}) collective-permute-start(bf16[16,4,16,128]{3,2,1,0:T(8,128)(2,1)S(1)} %get-tuple-element.36.refs_0_), channel_id=1, source_target_pairs={{0,192},{64,0},{128,64},{192,128},{1,193},{65,1},{129,65},{193,129... | collective-permute-start | bytes 786440 | tf_op jit(solution)/shard_map/ppermute | solution.py:300
  50.7 16.0 %collective-permute-start.2 = (bf16[16,4,16,128]{3,2,1,0:T(8,128)(2,1)S(1)}, bf16[16,4,16,128]{3,2,1,0:T(8,128)(2,1)S(1)}, u32[]{:S(2)}, u32[]{:S(2)}) collective-permute-start(bf16[16,4,16,128]{3,2,1,0:T(8,128)(2,1)S(1)} %get-tuple-element.36.refs_0_), channel_id=1, source_target_pairs={{0,128},{64,192},{128,0},{192,64},{1,129},{65,193},{129,1},{193,65... | collective-permute-start | bytes 786440 | tf_op jit(solution)/shard_map/ppermute | solution.py:300
  64.0 16.3 %collective-permute-start.14 = (bf16[4,2,16,1024]{3,2,1,0:T(8,128)(2,1)S(1)}, bf16[4,2,16,1024]{3,2,1,0:T(8,128)(2,1)S(1)}, u32[]{:S(2)}, u32[]{:S(2)}) collective-permute-start(bf16[4,2,16,1024]{3,2,1,0:T(8,128)(2,1)S(1)} %pad_maximum_fusion.refs_4_), channel_id=1, source_target_pairs={{0,56},{8,0},{16,8},{24,16},{32,24},{40,32},{48,40},{56,48},{1,57}... | collective-permute-start | bytes 786440 | tf_op jit(solution)/shard_map/ppermute | solution.py:310
  66.6 16.6 %collective-permute-start.15 = (bf16[4,2,16,1024]{3,2,1,0:T(8,128)(2,1)S(1)}, bf16[4,2,16,1024]{3,2,1,0:T(8,128)(2,1)S(1)}, u32[]{:S(2)}, u32[]{:S(2)}) collective-permute-start(bf16[4,2,16,1024]{3,2,1,0:T(8,128)(2,1)S(1)} %collective-permute-done.13.refs_5_), channel_id=1, source_target_pairs={{0,8},{8,16},{16,24},{24,32},{32,40},{40,48},{48,56},{56,0},{1,9},... | collective-permute-start | bytes 786440 | tf_op jit(solution)/shard_map/ppermute | solution.py:307
  66.7 3.4 %copy-start = (bf16[2,8,256,1024]{3,2,1,0:T(8,128)(2,1)S(1)}, bf16[2,8,256,1024]{3,2,1,0:T(8,128)(2,1)}, u32[]{:S(2)}) copy-start(bf16[2,8,256,1024]{3,2,1,0:T(8,128)(2,1)} %norm_media.1) | copy-start | bytes 25165828
  70.1 38.2 %copy-start.5 = (f32[2,1024]{1,0:T(2,128)S(1)}, f32[2,1024]{1,0:T(2,128)}, u32[]{:S(2)}) copy-start(f32[2,1024]{1,0:T(2,128)} %g_ref.7) | copy-start | bytes 24580
  77.0 9.0 %collective-permute-start.3 = (bf16[64,1024]{1,0:T(8,128)(2,1)S(1)}, bf16[64,1024]{1,0:T(8,128)(2,1)S(1)}, u32[]{:S(2)}, u32[]{:S(2)}) collective-permute-start(bf16[64,1024]{1,0:T(8,128)(2,1)S(1)} %get-tuple-element.23), channel_id=1, source_target_pairs={{0,1},{1,0},{2,3},{3,2},{4,5},{5,4},{6,7},{7,6},{8,9},{9,8},{10,11... | collective-permute-start | bytes 393224 | tf_op jit(solution)/shard_map/ppermute | solution.py:323
  80.3 8.3 %collective-permute-start.16 = (bf16[4,2,16,1024]{3,2,1,0:T(8,128)(2,1)S(1)}, bf16[4,2,16,1024]{3,2,1,0:T(8,128)(2,1)S(1)}, u32[]{:S(2)}, u32[]{:S(2)}) collective-permute-start(bf16[4,2,16,1024]{3,2,1,0:T(8,128)(2,1)S(1)} %collective-permute-done.14.refs_6_), channel_id=1, source_target_pairs={{0,56},{8,0},{16,8},{24,16},{32,24},{40,32},{48,40},{56,48},{1,57}... | collective-permute-start | bytes 786440 | tf_op jit(solution)/shard_map/ppermute | solution.py:310
  83.3 8.5 %collective-permute-start.17 = (bf16[4,2,16,1024]{3,2,1,0:T(8,128)(2,1)S(1)}, bf16[4,2,16,1024]{3,2,1,0:T(8,128)(2,1)S(1)}, u32[]{:S(2)}, u32[]{:S(2)}) collective-permute-start(bf16[4,2,16,1024]{3,2,1,0:T(8,128)(2,1)S(1)} %collective-permute-done.15.refs_7_), channel_id=1, source_target_pairs={{0,8},{8,16},{16,24},{24,32},{32,40},{40,48},{48,56},{56,0},{1,9},... | collective-permute-start | bytes 786440 | tf_op jit(solution)/shard_map/ppermute | solution.py:307
  83.3 17.6 %collective-permute-start.6 = (bf16[16,8,16,128]{3,2,1,0:T(8,128)(2,1)S(1)}, bf16[16,8,16,128]{3,2,1,0:T(8,128)(2,1)S(1)}, u32[]{:S(2)}, u32[]{:S(2)}) collective-permute-start(bf16[16,8,16,128]{3,2,1,0:T(8,128)(2,1)S(1)} %slice.21.refs_0_), channel_id=1, source_target_pairs={{0,64},{64,128},{128,192},{192,0},{1,65},{65,129},{129,193},{193,1... | collective-permute-start | bytes 1572872 | tf_op jit(solution)/shard_map/ppermute | solution.py:300
  83.7 17.1 %collective-permute-start.7 = (bf16[16,8,16,128]{3,2,1,0:T(8,128)(2,1)S(1)}, bf16[16,8,16,128]{3,2,1,0:T(8,128)(2,1)S(1)}, u32[]{:S(2)}, u32[]{:S(2)}) collective-permute-start(bf16[16,8,16,128]{3,2,1,0:T(8,128)(2,1)S(1)} %slice.21.refs_0_), channel_id=1, source_target_pairs={{0,192},{64,0},{128,64},{192,128},{1,193},{65,1},{129,65},{193,129... | collective-permute-start | bytes 1572872 | tf_op jit(solution)/shard_map/ppermute | solution.py:300
  86.1 22.2 %collective-permute-start.8 = (bf16[16,8,16,128]{3,2,1,0:T(8,128)(2,1)S(1)}, bf16[16,8,16,128]{3,2,1,0:T(8,128)(2,1)S(1)}, u32[]{:S(2)}, u32[]{:S(2)}) collective-permute-start(bf16[16,8,16,128]{3,2,1,0:T(8,128)(2,1)S(1)} %slice.21.refs_0_), channel_id=1, source_target_pairs={{0,128},{64,192},{128,0},{192,64},{1,129},{65,193},{129,1},{193,65... | collective-permute-start | bytes 1572872 | tf_op jit(solution)/shard_map/ppermute | solution.py:300
  88.6 4.1 %collective-permute-start.4 = (bf16[64,1024]{1,0:T(8,128)(2,1)S(1)}, bf16[64,1024]{1,0:T(8,128)(2,1)S(1)}, u32[]{:S(2)}, u32[]{:S(2)}) collective-permute-start(bf16[64,1024]{1,0:T(8,128)(2,1)S(1)} %add_convert_fusion.7), channel_id=1, source_target_pairs={{0,2},{2,0},{1,3},{3,1},{4,6},{6,4},{5,7},{7,5},{8,10},{10,8},{9,1... | collective-permute-start | bytes 393224 | tf_op jit(solution)/shard_map/ppermute | solution.py:325
  91.8 6.5 %collective-permute-start.18 = (bf16[4,2,16,1024]{3,2,1,0:T(8,128)(2,1)S(1)}, bf16[4,2,16,1024]{3,2,1,0:T(8,128)(2,1)S(1)}, u32[]{:S(2)}, u32[]{:S(2)}) collective-permute-start(bf16[4,2,16,1024]{3,2,1,0:T(8,128)(2,1)S(1)} %collective-permute-done.16.refs_8_), channel_id=1, source_target_pairs={{0,56},{8,0},{16,8},{24,16},{32,24},{40,32},{48,40},{56,48},{1,57}... | collective-permute-start | bytes 786440 | tf_op jit(solution)/shard_map/ppermute | solution.py:310
  92.7 8.1 %collective-permute-start.19 = (bf16[4,2,16,1024]{3,2,1,0:T(8,128)(2,1)S(1)}, bf16[4,2,16,1024]{3,2,1,0:T(8,128)(2,1)S(1)}, u32[]{:S(2)}, u32[]{:S(2)}) collective-permute-start(bf16[4,2,16,1024]{3,2,1,0:T(8,128)(2,1)S(1)} %collective-permute-done.17.refs_9_), channel_id=1, source_target_pairs={{0,8},{8,16},{16,24},{24,32},{32,40},{40,48},{48,56},{56,0},{1,9},... | collective-permute-start | bytes 786440 | tf_op jit(solution)/shard_map/ppermute | solution.py:307
  98.2 10.0 %collective-permute-start.5 = (bf16[64,1024]{1,0:T(8,128)(2,1)S(1)}, bf16[64,1024]{1,0:T(8,128)(2,1)S(1)}, u32[]{:S(2)}, u32[]{:S(2)}) collective-permute-start(bf16[64,1024]{1,0:T(8,128)(2,1)S(1)} %add_convert_fusion.6.mine_ref), channel_id=1, source_target_pairs={{0,1},{1,0},{2,3},{3,2},{4,5},{5,4},{6,7},{7,6},{8,9},{9,8},{10,11... | collective-permute-start | bytes 393224 | tf_op jit(solution)/shard_map/ppermute | solution.py:327
  110.7 3.0 %collective-permute-start.23 = (bf16[64,1024]{1,0:T(8,128)(2,1)S(1)}, bf16[64,1024]{1,0:T(8,128)(2,1)S(1)}, u32[]{:S(2)}, u32[]{:S(2)}) collective-permute-start(bf16[64,1024]{1,0:T(8,128)(2,1)S(1)} %get-tuple-element.27), channel_id=1, source_target_pairs={{0,1},{1,0},{2,3},{3,2},{4,5},{5,4},{6,7},{7,6},{8,9},{9,8},{10,11... | collective-permute-start | bytes 393224 | tf_op jit(solution)/shard_map/ppermute | solution.py:323
  113.7 5.2 %collective-permute-start.24 = (bf16[64,1024]{1,0:T(8,128)(2,1)S(1)}, bf16[64,1024]{1,0:T(8,128)(2,1)S(1)}, u32[]{:S(2)}, u32[]{:S(2)}) collective-permute-start(bf16[64,1024]{1,0:T(8,128)(2,1)S(1)} %add_convert_fusion.5), channel_id=1, source_target_pairs={{0,2},{2,0},{1,3},{3,1},{4,6},{6,4},{5,7},{7,5},{8,10},{10,8},{9,1... | collective-permute-start | bytes 393224 | tf_op jit(solution)/shard_map/ppermute | solution.py:325
  114.3 8.4 %collective-permute-start.20 = (bf16[16,4,16,128]{3,2,1,0:T(8,128)(2,1)S(1)}, bf16[16,4,16,128]{3,2,1,0:T(8,128)(2,1)S(1)}, u32[]{:S(2)}, u32[]{:S(2)}) collective-permute-start(bf16[16,4,16,128]{3,2,1,0:T(8,128)(2,1)S(1)} %get-tuple-element.35.refs_0_), channel_id=1, source_target_pairs={{0,64},{64,128},{128,192},{192,0},{1,65},{65,129},{129,193},{193,1... | collective-permute-start | bytes 786440 | tf_op jit(solution)/shard_map/ppermute | solution.py:300
  114.8 11.5 %collective-permute-start.21 = (bf16[16,4,16,128]{3,2,1,0:T(8,128)(2,1)S(1)}, bf16[16,4,16,128]{3,2,1,0:T(8,128)(2,1)S(1)}, u32[]{:S(2)}, u32[]{:S(2)}) collective-permute-start(bf16[16,4,16,128]{3,2,1,0:T(8,128)(2,1)S(1)} %get-tuple-element.35.refs_0_), channel_id=1, source_target_pairs={{0,192},{64,0},{128,64},{192,128},{1,193},{65,1},{129,65},{193,129... | collective-permute-start | bytes 786440 | tf_op jit(solution)/shard_map/ppermute | solution.py:300
  117.0 12.6 %collective-permute-start.22 = (bf16[16,4,16,128]{3,2,1,0:T(8,128)(2,1)S(1)}, bf16[16,4,16,128]{3,2,1,0:T(8,128)(2,1)S(1)}, u32[]{:S(2)}, u32[]{:S(2)}) collective-permute-start(bf16[16,4,16,128]{3,2,1,0:T(8,128)(2,1)S(1)} %get-tuple-element.35.refs_0_), channel_id=1, source_target_pairs={{0,128},{64,192},{128,0},{192,64},{1,129},{65,193},{129,1},{193,65... | collective-permute-start | bytes 786440 | tf_op jit(solution)/shard_map/ppermute | solution.py:300
  118.1 32.7 %collective-permute-start.29 = (bf16[16,16,16,128]{3,2,1,0:T(8,128)(2,1)S(1)}, bf16[16,16,16,128]{3,2,1,0:T(8,128)(2,1)S(1)}, u32[]{:S(2)}, u32[]{:S(2)}) collective-permute-start(bf16[16,16,16,128]{3,2,1,0:T(8,128)(2,1)S(1)} %all-to-all-done.1.refs_0_), channel_id=1, source_target_pairs={{0,64},{64,128},{128,192},{192,0},{1,65},{65,129},{129,193},{193,1... | collective-permute-start | bytes 3145736 | tf_op jit(solution)/shard_map/ppermute | solution.py:294
  119.0 31.9 %collective-permute-start.30 = (bf16[16,16,16,128]{3,2,1,0:T(8,128)(2,1)S(1)}, bf16[16,16,16,128]{3,2,1,0:T(8,128)(2,1)S(1)}, u32[]{:S(2)}, u32[]{:S(2)}) collective-permute-start(bf16[16,16,16,128]{3,2,1,0:T(8,128)(2,1)S(1)} %all-to-all-done.1.refs_0_), channel_id=1, source_target_pairs={{0,192},{64,0},{128,64},{192,128},{1,193},{65,1},{129,65},{193,129... | collective-permute-start | bytes 3145736 | tf_op jit(solution)/shard_map/ppermute | solution.py:294
  122.7 6.8 %collective-permute-start.25 = (bf16[64,1024]{1,0:T(8,128)(2,1)S(1)}, bf16[64,1024]{1,0:T(8,128)(2,1)S(1)}, u32[]{:S(2)}, u32[]{:S(2)}) collective-permute-start(bf16[64,1024]{1,0:T(8,128)(2,1)S(1)} %add_convert_fusion.4.refs_4_), channel_id=1, source_target_pairs={{0,1},{1,0},{2,3},{3,2},{4,5},{5,4},{6,7},{7,6},{8,9},{9,8},{10,11... | collective-permute-start | bytes 393224 | tf_op jit(solution)/shard_map/ppermute | solution.py:327
  129.6 3.4 %copy-start.1 = (bf16[2,8,256,1024]{3,2,1,0:T(8,128)(2,1)S(1)}, bf16[2,8,256,1024]{3,2,1,0:T(8,128)(2,1)}, u32[]{:S(2)}) copy-start(bf16[2,8,256,1024]{3,2,1,0:T(8,128)(2,1)} %norm_media.1) | copy-start | bytes 25165828
  139.9 38.0 %copy-start.6 = (f32[1024]{0:T(1024)S(1)}, f32[1024]{0:T(1024)}, u32[]{:S(2)}) copy-start(f32[1024]{0:T(1024)} %param.19) | copy-start | bytes 12292
  140.0 13.8 %collective-permute-start.26 = (bf16[64,1024]{1,0:T(8,128)(2,1)S(1)}, bf16[64,1024]{1,0:T(8,128)(2,1)S(1)}, u32[]{:S(2)}, u32[]{:S(2)}) collective-permute-start(bf16[64,1024]{1,0:T(8,128)(2,1)S(1)} %get-tuple-element.30), channel_id=1, source_target_pairs={{0,1},{1,0},{2,3},{3,2},{4,5},{5,4},{6,7},{7,6},{8,9},{9,8},{10,11... | collective-permute-start | bytes 393224 | tf_op jit(solution)/shard_map/ppermute | solution.py:323
  150.8 13.3 %collective-permute-start.31 = (bf16[8,16,16,128]{3,2,1,0:T(8,128)(2,1)S(1)}, bf16[8,16,16,128]{3,2,1,0:T(8,128)(2,1)S(1)}, u32[]{:S(2)}, u32[]{:S(2)}) collective-permute-start(bf16[8,16,16,128]{3,2,1,0:T(8,128)(2,1)S(1)} %slice.23), channel_id=1, source_target_pairs={{0,64},{64,128},{128,192},{192,0},{1,65},{65,129},{129,193},{193,1... | collective-permute-start | bytes 1572872 | tf_op jit(solution)/shard_map/ppermute | solution.py:295
  151.0 13.1 %collective-permute-start.32 = (bf16[8,16,16,128]{3,2,1,0:T(8,128)(2,1)S(1)}, bf16[8,16,16,128]{3,2,1,0:T(8,128)(2,1)S(1)}, u32[]{:S(2)}, u32[]{:S(2)}) collective-permute-start(bf16[8,16,16,128]{3,2,1,0:T(8,128)(2,1)S(1)} %slice.24), channel_id=1, source_target_pairs={{0,192},{64,0},{128,64},{192,128},{1,193},{65,1},{129,65},{193,129... | collective-permute-start | bytes 1572872 | tf_op jit(solution)/shard_map/ppermute | solution.py:295
  153.8 4.2 %collective-permute-start.27 = (bf16[64,1024]{1,0:T(8,128)(2,1)S(1)}, bf16[64,1024]{1,0:T(8,128)(2,1)S(1)}, u32[]{:S(2)}, u32[]{:S(2)}) collective-permute-start(bf16[64,1024]{1,0:T(8,128)(2,1)S(1)} %add_convert_fusion.3), channel_id=1, source_target_pairs={{0,2},{2,0},{1,3},{3,1},{4,6},{6,4},{5,7},{7,5},{8,10},{10,8},{9,1... | collective-permute-start | bytes 393224 | tf_op jit(solution)/shard_map/ppermute | solution.py:325
  158.0 4.0 %collective-permute-start.28 = (bf16[64,1024]{1,0:T(8,128)(2,1)S(1)}, bf16[64,1024]{1,0:T(8,128)(2,1)S(1)}, u32[]{:S(2)}, u32[]{:S(2)}) collective-permute-start(bf16[64,1024]{1,0:T(8,128)(2,1)S(1)} %add_convert_fusion.2.mine_ref), channel_id=1, source_target_pairs={{0,1},{1,0},{2,3},{3,2},{4,5},{5,4},{6,7},{7,6},{8,9},{9,8},{10,11... | collective-permute-start | bytes 393224 | tf_op jit(solution)/shard_map/ppermute | solution.py:327
  166.8 3.4 %collective-permute-start.33 = (bf16[64,1024]{1,0:T(8,128)(2,1)S(1)}, bf16[64,1024]{1,0:T(8,128)(2,1)S(1)}, u32[]{:S(2)}, u32[]{:S(2)}) collective-permute-start(bf16[64,1024]{1,0:T(8,128)(2,1)S(1)} %get-tuple-element.34), channel_id=1, source_target_pairs={{0,1},{1,0},{2,3},{3,2},{4,5},{5,4},{6,7},{7,6},{8,9},{9,8},{10,11... | collective-permute-start | bytes 393224 | tf_op jit(solution)/shard_map/ppermute | solution.py:323
  170.2 4.8 %collective-permute-start.34 = (bf16[64,1024]{1,0:T(8,128)(2,1)S(1)}, bf16[64,1024]{1,0:T(8,128)(2,1)S(1)}, u32[]{:S(2)}, u32[]{:S(2)}) collective-permute-start(bf16[64,1024]{1,0:T(8,128)(2,1)S(1)} %add_convert_fusion.1), channel_id=1, source_target_pairs={{0,2},{2,0},{1,3},{3,1},{4,6},{6,4},{5,7},{7,5},{8,10},{10,8},{9,1... | collective-permute-start | bytes 393224 | tf_op jit(solution)/shard_map/ppermute | solution.py:325
  175.1 2.3 %collective-permute-start.35 = (bf16[64,1024]{1,0:T(8,128)(2,1)S(1)}, bf16[64,1024]{1,0:T(8,128)(2,1)S(1)}, u32[]{:S(2)}, u32[]{:S(2)}) collective-permute-start(bf16[64,1024]{1,0:T(8,128)(2,1)S(1)} %add_convert_fusion), channel_id=1, source_target_pairs={{0,1},{1,0},{2,3},{3,2},{4,5},{5,4},{6,7},{7,6},{8,9},{9,8},{10,11... | collective-permute-start | bytes 393224 | tf_op jit(solution)/shard_map/ppermute | solution.py:327
